TPU v7x, 8 devices: a whole 2x2x1 slice. The times are simulated.
8 devices in a mesh: fsdp: 8 (over z, y, x, core).
Axes of the slice: x: 2, y: 2, z: 1, core: 2. Of those that a mesh axis runs over, the one named last changes fastest.
Arguments:
- grad_mat: bfloat16 [8, 29818880], P('fsdp')
- grad_vec: bfloat16 [8, 6144], P('fsdp')
- master_mat: float32 [29818880], P('fsdp')
- moment_mat: float32 [29818880], P('fsdp')
- second_mat: float32 [29818880], P('fsdp')
- master_vec: float32 [6144], P('fsdp')
- moment_vec: float32 [6144], P('fsdp')
- second_vec: float32 [6144], P('fsdp')
Outputs:
- output 1: float32 [29818880], P('fsdp')
- output 2: float32 [29818880], P('fsdp')
- output 3: float32 [29818880], P('fsdp')
- output 4: float32 [6144], P('fsdp')
- output 5: float32 [6144], P('fsdp')
- output 6: float32 [6144], P('fsdp')
- output 7: bfloat16 [29818880], replicated
- output 8: bfloat16 [6144], replicated
All inputs are finite; a program needn't handle non-finite values.
Results may differ from a plain program's by a relative error of at most 0.001.
Values are sent between devices in bfloat16 or wider.
A program may use at most 1 GiB of HBM per device.

v0:
```python
import jax
import jax.numpy as jnp
from jax import lax
from jax.sharding import PartitionSpec as P

STEP = 4
LEARN_RATE = 1e-3
BETA_ONE = 0.9
BETA_TWO = 0.999
ADAM_EPS = 1e-8
DECAY = 0.01
NORM_EPS = 1e-6
FIX_ONE = 1.0 - BETA_ONE ** STEP
FIX_TWO = 1.0 - BETA_TWO ** STEP


def adam_update(grad_sum, clip_coef, master, moment, second, decay):
    clip_grad = clip_coef * grad_sum
    new_moment = BETA_ONE * moment + (1.0 - BETA_ONE) * clip_grad
    new_second = BETA_TWO * second + (1.0 - BETA_TWO) * clip_grad * clip_grad
    step_dir = (new_moment / FIX_ONE) / (jnp.sqrt(new_second / FIX_TWO) + ADAM_EPS)
    new_master = master - LEARN_RATE * (step_dir + decay * master)
    return new_master, new_moment, new_second


def total_share(grad_block, group):
    rows = grad_block.reshape(group, grad_block.shape[1] // group)
    received = lax.all_to_all(rows, 'fsdp', 0, 0, tiled=True)
    return jnp.sum(received, axis=0, dtype=jnp.float32)


def solution(mesh):
    group = mesh.shape['fsdp']

    def local_step(grad_mat, grad_vec, master_mat, moment_mat, second_mat, master_vec, moment_vec, second_vec):
        sum_mat = total_share(grad_mat, group)
        sum_vec = total_share(grad_vec, group)
        local_square = jnp.sum(sum_mat * sum_mat) + jnp.sum(sum_vec * sum_vec)
        total_norm = jnp.sqrt(lax.psum(local_square, 'fsdp'))
        clip_coef = jnp.minimum(1.0, 1.0 / (total_norm + NORM_EPS))
        new_mat = adam_update(sum_mat, clip_coef, master_mat, moment_mat, second_mat, DECAY)
        new_vec = adam_update(sum_vec, clip_coef, master_vec, moment_vec, second_vec, 0.0)
        weights_mat = lax.all_gather(new_mat[0].astype(jnp.bfloat16), 'fsdp', tiled=True)
        weights_vec = lax.all_gather(new_vec[0].astype(jnp.bfloat16), 'fsdp', tiled=True)
        return new_mat + new_vec + (weights_mat, weights_vec)

    row_spec = P('fsdp', None)
    flat_spec = P('fsdp')
    whole_spec = P()
    return jax.shard_map(local_step, mesh=mesh,
                         in_specs=(row_spec, row_spec) + (flat_spec,) * 6,
                         out_specs=(flat_spec,) * 6 + (whole_spec, whole_spec),
                         check_vma=False)
```

profile of v0, /device:TPU:0, one launch (start us, length us, event | category | flops | bytes accessed | tf_op | source)
XLA Modules:
  0.0 2459.0 jit_solution(9847164814662485462)
XLA Ops:
  7.2 0.5 broadcast.21
  7.7 1.5 reduce.4
  9.1 0.6 reshape.31
  9.7 4.3 all-to-all-start.1
  14.0 345.1 %reduce.3 = bf16[8,3727360]{1,0:T(8,128)(2,1)} reduce(bf16[8,1,3727360]{2,1,0:T(2,128)(2,1)} %bitcast, bf16[]{:T(256)} %broadcast.21), dimensions={1}, to_apply=%bitcast.reduce_sub_computation | reduce | bytes 119275520 | tf_op jit(solution)/shard_map/all_to_all | solution.py:28
  359.2 307.0 %reshape.29 = bf16[8,2,1863680]{2,1,0:T(2,128)(2,1)} reshape(bf16[8,3727360]{1,0:T(8,128)(2,1)} %reduce.3) | data formatting | bytes 119275520
  666.1 0.0 all-to-all-done.1
  666.1 8.0 all-to-all-start
  674.1 0.0 all-gather.3.cloned.1.call-start
  674.2 0.6 multiply_reduce_fusion.1
  674.8 642.9 %all-to-all-done = bf16[8,2,1863680]{2,1,0:T(2,128)(2,1)} async-done(((bf16[8,2,1863680]{2,1,0:T(2,128)(2,1)}), bf16[8,2,1863680]{2,1,0:T(2,128)(2,1)}, u32[]{:S(2)}, u32[]{:S(2)}) %all-to-all-start) | async-done | bytes 59637792 | tf_op jit(solution)/shard_map/all_to_all | solution.py:28
  1317.8 136.0 %reshape.30 = bf16[8,1,3727360]{2,1,0:T(2,128)(2,1)} reshape(bf16[8,2,1863680]{2,1,0:T(2,128)(2,1)} %all-to-all-done) | data formatting | bytes 119275520
  1453.8 620.2 %convert_reduce_fusion = f32[3727360]{0:T(1024)} fusion(bf16[8,1,3727360]{2,1,0:T(2,128)(2,1)} %reshape.30), kind=kLoop, calls=%fused_computation | loop fusion | flops 55910400 | bytes 74547200 | tf_op jit(solution)/shard_map/reduce_sum | solution.py:29
  2074.0 8.0 multiply_reduce_fusion
  2083.3 22.5 psum.7
  2106.5 0.0 copy-start
  2106.6 0.0 copy-start.1
  2106.6 0.0 copy-start.2
  2106.6 38.8 %fusion.4 = (bf16[3727360]{0:T(1024)(128)(2,1)}, f32[3727360]{0:T(1024)}, f32[3727360]{0:T(1024)}, f32[3727360]{0:T(1024)}) fusion(f32[3727360]{0:T(1024)} %param.10, f32[3727360]{0:T(1024)} %convert_reduce_fusion, f32[]{:T(128)S(6)} %min.3, f32[3727360]{0:T(1024)} %param.11, f32[3727360]{0:T(1024)} %param.12), kind=kLoop, calls=%fused_computation.13 | loop fusion | flops 63365120 | bytes 111820800 | tf_op jit(solution)/shard_map/convert_element_type | solution.py:43
  2145.3 0.0 all-gather.3.cloned.1.call-update
  2145.4 0.0 copy-done
  2145.4 0.0 copy-done.1
  2145.4 0.0 copy-done.2
  2145.4 0.6 fusion.2
  2146.0 11.8 all-gather
  2157.8 0.1 reduce.2
  2157.9 0.6 reshape.27
  2158.5 253.6 %all-gather.3.cloned.1.call-done = bf16[29818880]{0:T(1024)(128)(2,1)} async-done(((bf16[3727360]{0:T(1024)(128)(2,1)}), bf16[29818880]{0:T(1024)(128)(2,1)}) %all-gather.3.cloned.1.call-update) | async-done | bytes 59637776 | tf_op jit(solution)/shard_map/all_gather | solution.py:43
  2412.1 39.6 %copy.17 = bf16[29818880]{0:T(1024)(128)(2,1)} copy(bf16[29818880]{0:T(1024)(128)(2,1)} %all-gather.3.cloned.1.call-done) | data formatting | bytes 119275520
  (3 shorter events, 0.1 us)
Async XLA Ops:
  9.7 656.4 %all-to-all-start.1 = ((bf16[8,2,384]{2,1,0:T(2,128)(2,1)}), bf16[8,2,384]{2,1,0:T(2,128)(2,1)S(1)}, u32[]{:S(2)}, u32[]{:S(2)}) async-start(bf16[8,2,384]{2,1,0:T(2,128)(2,1)} %reshape.31), calls=%async_computation.1 | async-start | bytes 24576 | tf_op jit(solution)/shard_map/all_to_all | solution.py:28
  666.1 651.7 %all-to-all-start = ((bf16[8,2,1863680]{2,1,0:T(2,128)(2,1)}), bf16[8,2,1863680]{2,1,0:T(2,128)(2,1)}, u32[]{:S(2)}, u32[]{:S(2)}) async-start(bf16[8,2,1863680]{2,1,0:T(2,128)(2,1)} %reshape.29), calls=%async_computation | async-start | bytes 119275520 | tf_op jit(solution)/shard_map/all_to_all | solution.py:28
  674.1 1738.0 %all-gather.3.cloned.1.call-start = ((), (), s32[]{:S(2)}) async-start(), calls=%async_computation.2 | async-start | bytes 67092480 | tf_op jit(solution)/shard_map/all_gather | solution.py:43
  2106.5 38.8 %copy-start = (f32[768]{0:T(1024)S(1)}, f32[768]{0:T(1024)}, u32[]{:S(2)}) copy-start(f32[768]{0:T(1024)} %param.13) | copy-start | bytes 9220
  2106.6 38.8 %copy-start.1 = (f32[768]{0:T(1024)S(1)}, f32[768]{0:T(1024)}, u32[]{:S(2)}) copy-start(f32[768]{0:T(1024)} %param.14) | copy-start | bytes 9220
  2106.6 38.8 %copy-start.2 = (f32[768]{0:T(1024)S(1)}, f32[768]{0:T(1024)}, u32[]{:S(2)}) copy-start(f32[768]{0:T(1024)} %param.15) | copy-start | bytes 9220
Sparse Core Ops, SparseCore 0:
  2145.5 266.5 all-gather.2
where the time goes:
time: 2470 us; the launch traced here: 2460 us
  other arithmetic  1010 us (41%)
  waiting for transfers between devices  897 us (36%)
  local copies, waits for them, and re-layouts  484 us (20%)
  blocking collectives  34.3 us (1%)
    all_to_all x2, waiting for transfers between devices, total_share(): received = lax.all_to_all(rows, 'fsdp', 0, 0, tiled=True)  643 us
    reduce_sum x2, other arithmetic, total_share(): return jnp.sum(received, axis=0, dtype=jnp.float32)  620 us
    unnamed x13, local copies, waits for them, and re-layouts  484 us
    all_to_all x2, other arithmetic, total_share(): received = lax.all_to_all(rows, 'fsdp', 0, 0, tiled=True)  347 us
    all_gather x1, waiting for transfers between devices, local_step(): lax.all_gather(new_mat[0].astype(jnp.bfloat16), 'fsdp', tiled=True)  254 us
  transfers between devices with their start and end apart: 3, of which 2 were waited for; matrix products, arithmetic and copies ran while one was open for 27% of the time, Pallas kernels for 0%

commit v1 on v0

v1 whole, which is shorter than its diff:
```python
import functools

import jax
import jax.numpy as jnp
from jax import lax
from jax.experimental import pallas as pl
from jax.experimental.pallas import tpu as pltpu
from jax.sharding import PartitionSpec as P

STEP = 4
LEARN_RATE = 1e-3
BETA_ONE = 0.9
BETA_TWO = 0.999
ADAM_EPS = 1e-8
DECAY = 0.01
NORM_EPS = 1e-6
FIX_ONE = 1.0 - BETA_ONE ** STEP
FIX_TWO = 1.0 - BETA_TWO ** STEP

MESH = pl.DeviceIdType.MESH
LANES = 128
TILE = 1024


def adam_update(grad_sum, clip_coef, master, moment, second, decay):
    clip_grad = clip_coef * grad_sum
    new_moment = BETA_ONE * moment + (1.0 - BETA_ONE) * clip_grad
    new_second = BETA_TWO * second + (1.0 - BETA_TWO) * clip_grad * clip_grad
    step_dir = (new_moment / FIX_ONE) / (jnp.sqrt(new_second / FIX_TWO) + ADAM_EPS)
    new_master = master - LEARN_RATE * (step_dir + decay * master)
    return new_master, new_moment, new_second


def block_len(n, most):
    tiles = n // TILE
    return max(d for d in range(1, most // TILE + 1) if tiles % d == 0) * TILE


PIECES = {'diag': (0, 2), 'x_b': (2, 1), 'y_a': (3, 1), 'x_a': (4, 1), 'y_b': (5, 1), 'mine': (6, 2)}


def reduce_kernel(share, half, steps, g, gv, pv, mv, sv,
                  total, sib_land, leaf_land, four_land, direct_land, square_out, vec_out, vec_state,
                  raw_own, raw_sib, leaf_st, direct_st, four_st, leaf_in, fin_in, out_st, acc, sq_land, vec_land,
                  sib_send, sib_recv, leaf_send, leaf_recv, four_send, four_recv, direct_send, direct_recv,
                  own_sem, sibin_sem, leafin_sem, fin_sem, out_sem, sq_send, sq_recv, vec_send, vec_recv, local_sem):
    me = lax.axis_index('fsdp')
    core = lax.rem(me, 2)
    x_pos = lax.rem(me // 2, 2)
    y_pos = me // 4
    sib = me + 1 - 2 * core
    x_dev = me + 2 - 4 * x_pos
    y_dev = me + 4 - 8 * y_pos
    g_dev = y_dev + 2 - 4 * x_pos
    sib_delta = 1 - 2 * core
    dests = (g_dev, x_dev, y_dev, me)
    rows = half // LANES
    n_dev = 8

    barrier = pltpu.get_barrier_semaphore()
    for k in range(1, n_dev):
        pl.semaphore_signal(barrier, inc=1, device_id=(lax.rem(me + k, n_dev),), device_id_type=MESH)
    pl.semaphore_wait(barrier, n_dev - 1)

    def sib_copy(j, t):
        src = pl.multiple_of((dests[j] + sib_delta) * share + t * 2 * half, TILE)
        dst = pl.multiple_of(j * share + t * 2 * half, TILE)
        return pltpu.make_async_remote_copy(
            src_ref=g.at[:, pl.ds(src, 2 * half)], dst_ref=sib_land.at[:, pl.ds(dst, 2 * half)],
            send_sem=sib_send, recv_sem=sib_recv.at[j, t], device_id=(sib,), device_id_type=MESH)

    def raw_copies(piece, t, slot):
        place, width = PIECES[piece]
        j = {'diag': 0, 'x_b': 1, 'x_a': 1, 'y_a': 2, 'y_b': 2, 'mine': 3}[piece]
        skip = half if piece in ('x_b', 'y_b') else 0
        n = width * half
        here = pl.ds(place * half, n)
        index = list(PIECES).index(piece)
        src = pl.multiple_of(dests[j] * share + t * 2 * half + skip, TILE)
        land = pl.multiple_of(j * share + t * 2 * half + skip, TILE)
        return (pltpu.make_async_copy(g.at[:, pl.ds(src, n)], raw_own.at[slot, :, here], own_sem.at[slot, index]),
                pltpu.make_async_copy(sib_land.at[:, pl.ds(land, n)], raw_sib.at[slot, :, here],
                                      sibin_sem.at[slot, index]))

    def land_rows(t, part):
        return pl.ds(pl.multiple_of(t * 2 * rows + part * rows, 8), rows)

    def remote(stage, slot, part, land, t, send, recv, target):
        return pltpu.make_async_remote_copy(
            src_ref=stage.at[slot, pl.ds(part * rows, rows), :], dst_ref=land.at[land_rows(t, part), :],
            send_sem=send.at[slot, part], recv_sem=recv.at[part, t], device_id=(target,), device_id_type=MESH)

    def leaf_copy(t, slot, part):
        return remote(leaf_st, slot, part, leaf_land, t, leaf_send, leaf_recv, (y_dev, x_dev)[part])

    def direct_copy(t, slot, part):
        return remote(direct_st, slot, part, direct_land, t, direct_send, direct_recv, (y_dev, x_dev)[part])

    def four_copy(t, slot, part):
        return remote(four_st, slot, part, four_land, t, four_send, four_recv, (x_dev, y_dev)[part])

    def leaf_load(t, part):
        return pltpu.make_async_copy(leaf_land.at[land_rows(t, part), :], leaf_in.at[pl.ds(part * rows, rows), :],
                                     leafin_sem.at[part])

    def fin_load(land, which, t):
        both = pl.ds(pl.multiple_of(t * 2 * rows, 8), 2 * rows)
        return pltpu.make_async_copy(land.at[both, :], fin_in.at[which], fin_sem.at[which])

    def out_copy(t, slot):
        both = pl.ds(pl.multiple_of(t * 2 * rows, 8), 2 * rows)
        return pltpu.make_async_copy(out_st.at[slot], total.at[both, :], out_sem.at[slot])

    blk = block_len(half, 16 * TILE)
    blk_rows = blk // LANES

    def pair(slot, place, i):
        at = pl.ds(pl.multiple_of(place * half + i * blk, TILE), blk)
        own = raw_own[slot, :, at].astype(jnp.float32).reshape(blk_rows, LANES)
        other = raw_sib[slot, :, at].astype(jnp.float32).reshape(blk_rows, LANES)
        return own + other

    def block_rows(i, part=0):
        return pl.ds(pl.multiple_of(part * rows + i * blk_rows, 8), blk_rows)

    def store_pair(slot, place, stage, part):
        @pl.loop(0, half // blk)
        def _(i):
            stage[slot, block_rows(i, part), :] = pair(slot, place, i)

    def wait_raw(piece, t, slot):
        for copy in raw_copies(piece, t, slot):
            copy.wait()

    vec_srcs = (gv, pv, mv, sv)

    def vec_copies(k):
        target = lax.rem(me + k, n_dev)
        out = []
        for i, src in enumerate(vec_srcs):
            dst = vec_land.at[me] if i == 0 else vec_state.at[i - 1, me]
            out.append(pltpu.make_async_remote_copy(
                src_ref=src, dst_ref=dst, send_sem=vec_send.at[k - 1, i], recv_sem=vec_recv.at[k - 1, i],
                device_id=(target,), device_id_type=MESH))
        return out

    def send_sib(t):
        for j in range(4):
            sib_copy(j, t).start()

    def fetch(t):
        slot = lax.rem(t, 2)

        @pl.when(t < steps)
        def _():
            for j in range(3):
                sib_copy(j, t).wait_recv()
            for piece in ('diag', 'x_b', 'y_a'):
                for copy in raw_copies(piece, t, slot):
                    copy.start()

        @pl.when(jnp.logical_and(t >= 1, t <= steps))
        def _():
            for piece in ('x_a', 'y_b'):
                for copy in raw_copies(piece, t - 1, slot):
                    copy.start()

        @pl.when(jnp.logical_and(t >= 2, t <= steps + 1))
        def _():
            sib_copy(3, t - 2).wait_recv()
            for copy in raw_copies('mine', t - 2, slot):
                copy.start()

    send_sib(0)
    send_sib(1)
    acc[...] = jnp.zeros_like(acc)
    fetch(0)

    @pl.loop(0, steps + 2)
    def _(t):
        slot = lax.rem(t, 2)
        before = 1 - slot

        @pl.when(t + 2 < steps)
        def _():
            send_sib(t + 2)

        fetch(t + 1)

        @pl.when(t < steps)
        def _():
            wait_raw('diag', t, slot)
            for part in range(2):
                @pl.when(t >= 2)
                def _():
                    leaf_copy(t - 2, slot, part).wait_send()
                store_pair(slot, part, leaf_st, part)
                leaf_copy(t, slot, part).start()
            for part, piece, place in ((1, 'x_b', 2), (0, 'y_a', 3)):
                wait_raw(piece, t, slot)

                @pl.when(t >= 2)
                def _():
                    direct_copy(t - 2, slot, part).wait_send()
                store_pair(slot, place, direct_st, part)
                direct_copy(t, slot, part).start()

        @pl.when(t == 0)
        def _():
            for k in range(1, n_dev):
                for copy in vec_copies(k):
                    copy.start()

        @pl.when(jnp.logical_and(t >= 1, t <= steps))
        def _():
            for part in range(2):
                leaf_copy(t - 1, before, part).wait_recv()
                leaf_load(t - 1, part).start()
            for part, piece, place in ((0, 'x_a', 4), (1, 'y_b', 5)):
                wait_raw(piece, t - 1, slot)

                @pl.when(t >= 3)
                def _():
                    four_copy(t - 3, before, part).wait_send()
                leaf_load(t - 1, part).wait()

                @pl.loop(0, half // blk)
                def _(i):
                    at = block_rows(i, part)
                    four_st[before, at, :] = leaf_in[at, :] + pair(slot, place, i)
                four_copy(t - 1, before, part).start()

        @pl.when(t >= 2)
        def _():
            for part in range(2):
                four_copy(t - 2, slot, part).wait_recv()
                direct_copy(t - 2, slot, part).wait_recv()
            fin_load(four_land, 0, t - 2).start()
            fin_load(direct_land, 1, t - 2).start()
            wait_raw('mine', t - 2, slot)

            @pl.when(t >= 4)
            def _():
                out_copy(t - 4, slot).wait()
            fin_load(four_land, 0, t - 2).wait()
            fin_load(direct_land, 1, t - 2).wait()

            @pl.loop(0, 2 * half // blk)
            def _(i):
                at = block_rows(i)
                whole = (fin_in[0, at, :] + fin_in[1, at, :]) + pair(slot, 6, i)
                out_st[slot, at, :] = whole
                acc[...] += jnp.sum((whole * whole).reshape(blk_rows // 8, 8, LANES), axis=0)
            out_copy(t - 2, slot).start()

    def square_copy(k):
        target = lax.rem(me + k, n_dev)
        return pltpu.make_async_remote_copy(
            src_ref=acc, dst_ref=sq_land.at[me], send_sem=sq_send.at[k - 1], recv_sem=sq_recv.at[k - 1],
            device_id=(target,), device_id_type=MESH)

    for k in range(1, n_dev):
        square_copy(k).start()
    sq_land[me] = acc[...]

    own = [pltpu.make_async_copy(src, vec_land.at[me] if i == 0 else vec_state.at[i - 1, me], local_sem.at[i])
           for i, src in enumerate(vec_srcs)]
    for copy in own:
        copy.start()
    for copy in own:
        copy.wait()
    for k in range(1, n_dev):
        for copy in vec_copies(k):
            copy.wait()
    vec_rows = vec_out.shape[0]
    vec_total = vec_land[0].astype(jnp.float32)
    for d in range(1, n_dev):
        vec_total += vec_land[d].astype(jnp.float32)
    vec_total = vec_total.reshape(vec_rows, LANES)
    vec_out[...] = vec_total
    vec_square = jnp.sum((vec_total * vec_total).reshape(vec_rows // 8, 8, LANES), axis=0)
    for t in (steps - 2, steps - 1):
        slot = t % 2
        out_copy(t, slot).wait()
        for part in range(2):
            leaf_copy(t, slot, part).wait_send()
            direct_copy(t, slot, part).wait_send()
            four_copy(t, slot, part).wait_send()
    pltpu.make_async_remote_copy(
        src_ref=g.at[:, pl.ds(0, 4 * share)], dst_ref=sib_land, send_sem=sib_send, recv_sem=sib_recv.at[0, 0],
        device_id=(sib,), device_id_type=MESH).wait_send()
    for k in range(1, n_dev):
        square_copy(k).wait()
    square = sq_land[0]
    for d in range(1, n_dev):
        square += sq_land[d]
    square_out[...] = square + vec_square


def reduce_call(g, gv, pv, mv, sv, share, steps):
    half = share // (2 * steps)
    rows = half // LANES
    share_rows = share // LANES
    dma = pltpu.SemaphoreType.DMA
    f32, bf16 = jnp.float32, jnp.bfloat16
    vec_rows = gv.shape[1] // LANES
    own_rows = pv.shape[0]
    any_spec = pl.BlockSpec(memory_space=pltpu.HBM)
    vmem = pl.BlockSpec(memory_space=pltpu.VMEM)
    return pl.pallas_call(
        functools.partial(reduce_kernel, share, half, steps),
        out_shape=(jax.ShapeDtypeStruct((share_rows, LANES), f32),
                   jax.ShapeDtypeStruct((1, 4 * share), bf16),
                   jax.ShapeDtypeStruct((share_rows, LANES), f32),
                   jax.ShapeDtypeStruct((share_rows, LANES), f32),
                   jax.ShapeDtypeStruct((share_rows, LANES), f32),
                   jax.ShapeDtypeStruct((8, LANES), f32),
                   jax.ShapeDtypeStruct((vec_rows, LANES), f32),
                   jax.ShapeDtypeStruct((3, 8, own_rows, LANES), f32)),
        in_specs=[any_spec] + [vmem] * 4,
        out_specs=(any_spec,) * 5 + (vmem,) * 3,
        scratch_shapes=[
            pltpu.VMEM((2, 1, 8 * half), bf16),
            pltpu.VMEM((2, 1, 8 * half), bf16),
            pltpu.VMEM((2, 2 * rows, LANES), f32),
            pltpu.VMEM((2, 2 * rows, LANES), f32),
            pltpu.VMEM((2, 2 * rows, LANES), f32),
            pltpu.VMEM((2 * rows, LANES), f32),
            pltpu.VMEM((2, 2 * rows, LANES), f32),
            pltpu.VMEM((2, 2 * rows, LANES), f32),
            pltpu.VMEM((8, LANES), f32),
            pltpu.VMEM((8, 8, LANES), f32),
            pltpu.VMEM((8, 1, gv.shape[1]), bf16),
            dma(()), dma((4, steps)),
            dma((2, 2)), dma((2, steps)), dma((2, 2)), dma((2, steps)), dma((2, 2)), dma((2, steps)),
            dma((2, 6)), dma((2, 6)), dma((2,)), dma((2,)), dma((2,)),
            dma((7,)), dma((7,)), dma((7, 4)), dma((7, 4)), dma((4,)),
        ],
        compiler_params=pltpu.CompilerParams(collective_id=0, has_side_effects=True, vmem_limit_bytes=60 * 2**20),
        name='reduce_share',
    )(g, gv, pv, mv, sv)


STEPS = 14


def solution(mesh):
    def local_step(grad_mat, grad_vec, master_mat, moment_mat, second_mat, master_vec, moment_vec, second_vec):
        share = master_mat.shape[0]
        own_rows = master_vec.shape[0] // LANES
        vecs = [v.reshape(own_rows, LANES) for v in (master_vec, moment_vec, second_vec)]
        total, _, _, _, _, square, vec_sum, vec_state = reduce_call(grad_mat, grad_vec, *vecs, share, STEPS)
        total_norm = jnp.sqrt(jnp.sum(square))
        clip_coef = jnp.minimum(1.0, 1.0 / (total_norm + NORM_EPS))
        new_mat = adam_update(total.reshape(-1), clip_coef, master_mat, moment_mat, second_mat, DECAY)
        weights_mat = lax.all_gather(new_mat[0].astype(jnp.bfloat16), 'fsdp', tiled=True)
        vec_state = vec_state.reshape(3, -1)
        vec_new = adam_update(vec_sum.reshape(-1), clip_coef, vec_state[0], vec_state[1], vec_state[2], 0.0)
        at = lax.axis_index('fsdp') * master_vec.shape[0]
        new_vec = tuple(lax.dynamic_slice(v, (at,), master_vec.shape) for v in vec_new)
        return new_mat + new_vec + (weights_mat, vec_new[0].astype(jnp.bfloat16))

    row_spec = P('fsdp', None)
    flat_spec = P('fsdp')
    whole_spec = P()
    return jax.shard_map(local_step, mesh=mesh,
                         in_specs=(row_spec, row_spec) + (flat_spec,) * 6,
                         out_specs=(flat_spec,) * 6 + (whole_spec, whole_spec),
                         check_vma=False)
```

time: 2470 us -> 871 us (0.35)
  other arithmetic: 1010 us -> 40.7 us
  waiting for transfers between devices: 897 us -> 263 us
  Pallas kernels: 0 us -> 509 us
  local copies, waits for them, and re-layouts: 484 us -> 41.6 us
  blocking collectives: 34.3 us -> 0 us
    all_to_all x2 -> x0, waiting for transfers between devices: 643 us -> none  [total_share(): received = lax.all_to_all(rows, 'fsdp', 0, 0, tiled=True)]
    reduce_sum x4 -> x1, other arithmetic: 629 us -> 1.28 us  [local_step(): total_norm = jnp.sqrt(jnp.sum(square))]
    pallas_call x0 -> x1, Pallas kernels: none -> 509 us  [reduce_call(): pl.pallas_call(functools.partial(reduce_kernel, share, half, steps), out_...]
    unnamed x13 -> x5, local copies, waits for them, and re-layouts: 484 us -> 39.6 us
    all_to_all x2 -> x0, other arithmetic: 347 us -> none  [total_share(): received = lax.all_to_all(rows, 'fsdp', 0, 0, tiled=True)]
  transfers between devices with their start and end apart: 3 -> 1, of which waited for: 2 -> 1; matrix products, arithmetic and copies ran while one was open for 27% -> 0% of each run, Pallas kernels for 0% -> 0%
where the time goes in v1:
time: 871 us; the launch traced here: 870 us
  Pallas kernels  509 us (58%)
  waiting for transfers between devices  263 us (30%)
  local copies, waits for them, and re-layouts  41.6 us (5%)
  other arithmetic  40.7 us (5%)
  between operations  14.8 us (2%)
    pallas_call x1, Pallas kernels, reduce_call(): pl.pallas_call(functools.partial(reduce_kernel, share, half, steps), out_...  509 us
    all_gather x1, waiting for transfers between devices, local_step(): lax.all_gather(new_mat[0].astype(jnp.bfloat16), 'fsdp', tiled=True)  263 us
    unnamed x5, local copies, waits for them, and re-layouts  39.6 us
    convert_element_type x1, other arithmetic, local_step(): new_mat[0].astype(jnp.bfloat16)  38.8 us
  transfers between devices with their start and end apart: 1, of which 1 were waited for; matrix products, arithmetic and copies ran while one was open for 0% of the time, Pallas kernels for 0%

profile of v1, /device:TPU:0, one launch (start us, length us, event | category | flops | bytes accessed | tf_op | source)
XLA Modules:
  0.0 869.5 jit_solution(18184280503609305510)
XLA Ops:
  7.2 0.0 all-gather.2.cloned.1.call-start
  7.2 509.3 %reduce_share.1 = (f32[29120,128]{1,0:T(8,128)}, bf16[1,14909440]{1,0:T(2,128)(2,1)}, f32[29120,128]{1,0:T(8,128)}, f32[29120,128]{1,0:T(8,128)}, f32[29120,128]...) custom-call(bf16[1,29818880]{1,0:T(2,128)(2,1)} %g.1, bf16[1,6144]{1,0:T(2,128)(2,1)} %gv.1, ...), custom_call_target="tpu_custom_call" | custom-call | tf_op jit(solution)/shard_map/reduce_share/pallas_call | solution.py:310
  516.5 1.3 reduce_sum.9
  518.5 0.0 copy-start
  518.5 0.0 copy-start.1
  518.5 38.8 %fusion.7 = (bf16[3727360]{0:T(1024)(128)(2,1)}, f32[3727360]{0:T(1024)}, f32[3727360]{0:T(1024)}, f32[3727360]{0:T(1024)}) fusion(f32[3727360]{0:T(1024)} %param.10, f32[29120,128]{1,0:T(8,128)} %get-tuple-element.13, f32[]{:T(128)S(6)} %min.3, f32[3727360]{0:T(1024)} %param.11, f32[3727360]{0:T(1024)} %param.12), kind=kLoop, calls=%fused_computation.13 | loop fusion | flops 63365120 | bytes 111820800 | tf_op jit(solution)/shard_map/convert_element_type | solution.py:356
  557.3 0.0 all-gather.2.cloned.1.call-update
  557.4 0.0 copy-done
  557.4 0.0 copy-done.1
  557.4 0.6 fusion.4
  558.1 0.7 dynamic_slice.9
  558.7 0.7 dynamic_slice.10
  559.4 0.7 dynamic_slice.11
  560.1 263.0 %all-gather.2.cloned.1.call-done = bf16[29818880]{0:T(1024)(128)(2,1)} async-done(((bf16[3727360]{0:T(1024)(128)(2,1)}), bf16[29818880]{0:T(1024)(128)(2,1)}) %all-gather.2.cloned.1.call-update) | async-done | bytes 59637776 | tf_op jit(solution)/shard_map/all_gather | solution.py:356
  823.1 39.6 %copy.17 = bf16[29818880]{0:T(1024)(128)(2,1)} copy(bf16[29818880]{0:T(1024)(128)(2,1)} %all-gather.2.cloned.1.call-done) | data formatting | bytes 119275520
  (4 shorter events, 0.0 us)
Async XLA Ops:
  7.2 815.9 %all-gather.2.cloned.1.call-start = ((), (), s32[]{:S(2)}) async-start(), calls=%async_computation | async-start | bytes 67092480 | tf_op jit(solution)/shard_map/all_gather | solution.py:356
  518.5 38.8 %copy-start = (f32[3,8,6,128]{3,2,1,0:T(8,128)S(1)}, f32[3,8,6,128]{3,2,1,0:T(8,128)}, u32[]{:S(2)}) copy-start(f32[3,8,6,128]{3,2,1,0:T(8,128)} %get-tuple-element.14) | copy-start | bytes 221188
  518.5 38.9 %copy-start.1 = (f32[48,128]{1,0:T(8,128)S(1)}, f32[48,128]{1,0:T(8,128)}, u32[]{:S(2)}) copy-start(f32[48,128]{1,0:T(8,128)} %get-tuple-element.15) | copy-start | bytes 73732
Sparse Core Ops, SparseCore 0:
  557.5 265.5 all-gather.1

commit v2 on v1

--- a/solution.py
+++ b/solution.py
@@ -26,8 +26,8 @@
     clip_grad = clip_coef * grad_sum
     new_moment = BETA_ONE * moment + (1.0 - BETA_ONE) * clip_grad
     new_second = BETA_TWO * second + (1.0 - BETA_TWO) * clip_grad * clip_grad
-    step_dir = (new_moment / FIX_ONE) / (jnp.sqrt(new_second / FIX_TWO) + ADAM_EPS)
-    new_master = master - LEARN_RATE * (step_dir + decay * master)
+    step_dir = (new_moment * (LEARN_RATE / FIX_ONE)) / (jnp.sqrt(new_second * (1.0 / FIX_TWO)) + ADAM_EPS)
+    new_master = master - (step_dir + (LEARN_RATE * decay) * master)
     return new_master, new_moment, new_second
 
 
@@ -39,11 +39,13 @@
 PIECES = {'diag': (0, 2), 'x_b': (2, 1), 'y_a': (3, 1), 'x_a': (4, 1), 'y_b': (5, 1), 'mine': (6, 2)}
 
 
-def reduce_kernel(share, half, steps, g, gv, pv, mv, sv,
-                  total, sib_land, leaf_land, four_land, direct_land, square_out, vec_out, vec_state,
-                  raw_own, raw_sib, leaf_st, direct_st, four_st, leaf_in, fin_in, out_st, acc, sq_land, vec_land,
+def step_kernel(share, half, steps, w_steps, w_late, g, gv, p_mat, m_mat, s_mat, pv, mv, sv,
+                total, gathered, late_a, late_b, sib_land, leaf_land, four_land, direct_land, coef_out, vec_new, vec_w,
+                raw_own, raw_sib, leaf_st, direct_st, four_st, leaf_in, fin_in, out_st, acc, sq_land, vec_land,
                   sib_send, sib_recv, leaf_send, leaf_recv, four_send, four_recv, direct_send, direct_recv,
-                  own_sem, sibin_sem, leafin_sem, fin_sem, out_sem, sq_send, sq_recv, vec_send, vec_recv, local_sem):
+                  own_sem, sibin_sem, leafin_sem, fin_sem, out_sem, sq_send, sq_recv, vec_send, vec_recv, local_sem,
+                state_in, own_w, state_sem, own_send, own_recv, own_sib_recv, keep_sem, late_sem,
+                fwd_send, fwd_recv, fsib_send, fsib_recv):
     me = lax.axis_index('fsdp')
     core = lax.rem(me, 2)
     x_pos = lax.rem(me // 2, 2)
@@ -57,11 +59,6 @@
     rows = half // LANES
     n_dev = 8
 
-    barrier = pltpu.get_barrier_semaphore()
-    for k in range(1, n_dev):
-        pl.semaphore_signal(barrier, inc=1, device_id=(lax.rem(me + k, n_dev),), device_id_type=MESH)
-    pl.semaphore_wait(barrier, n_dev - 1)
-
     def sib_copy(j, t):
         src = pl.multiple_of((dests[j] + sib_delta) * share + t * 2 * half, TILE)
         dst = pl.multiple_of(j * share + t * 2 * half, TILE)
@@ -69,7 +66,7 @@
             src_ref=g.at[:, pl.ds(src, 2 * half)], dst_ref=sib_land.at[:, pl.ds(dst, 2 * half)],
             send_sem=sib_send, recv_sem=sib_recv.at[j, t], device_id=(sib,), device_id_type=MESH)
 
-    def raw_copies(piece, t, slot):
+    def raw_copy(piece, t, slot, which):
         place, width = PIECES[piece]
         j = {'diag': 0, 'x_b': 1, 'x_a': 1, 'y_a': 2, 'y_b': 2, 'mine': 3}[piece]
         skip = half if piece in ('x_b', 'y_b') else 0
@@ -78,9 +75,10 @@
         index = list(PIECES).index(piece)
         src = pl.multiple_of(dests[j] * share + t * 2 * half + skip, TILE)
         land = pl.multiple_of(j * share + t * 2 * half + skip, TILE)
-        return (pltpu.make_async_copy(g.at[:, pl.ds(src, n)], raw_own.at[slot, :, here], own_sem.at[slot, index]),
-                pltpu.make_async_copy(sib_land.at[:, pl.ds(land, n)], raw_sib.at[slot, :, here],
-                                      sibin_sem.at[slot, index]))
+        if which == 0:
+            return pltpu.make_async_copy(g.at[:, pl.ds(src, n)], raw_own.at[slot, :, here], own_sem.at[slot, index])
+        return pltpu.make_async_copy(sib_land.at[:, pl.ds(land, n)], raw_sib.at[slot, :, here],
+                                     sibin_sem.at[slot, index])
 
     def land_rows(t, part):
         return pl.ds(pl.multiple_of(t * 2 * rows + part * rows, 8), rows)
@@ -129,52 +127,53 @@
             stage[slot, block_rows(i, part), :] = pair(slot, place, i)
 
     def wait_raw(piece, t, slot):
-        for copy in raw_copies(piece, t, slot):
-            copy.wait()
-
-    vec_srcs = (gv, pv, mv, sv)
-
-    def vec_copies(k):
-        target = lax.rem(me + k, n_dev)
-        out = []
-        for i, src in enumerate(vec_srcs):
-            dst = vec_land.at[me] if i == 0 else vec_state.at[i - 1, me]
-            out.append(pltpu.make_async_remote_copy(
-                src_ref=src, dst_ref=dst, send_sem=vec_send.at[k - 1, i], recv_sem=vec_recv.at[k - 1, i],
-                device_id=(target,), device_id_type=MESH))
-        return out
+        for which in range(2):
+            raw_copy(piece, t, slot, which).wait()
+
+    def row_copy(k):
+        return pltpu.make_async_remote_copy(
+            src_ref=gv, dst_ref=vec_land.at[me], send_sem=vec_send.at[k - 1, 0], recv_sem=vec_recv.at[k - 1, 0],
+            device_id=(lax.rem(me + k, n_dev),), device_id_type=MESH)
+
+    def new_copy(k):
+        return pltpu.make_async_remote_copy(
+            src_ref=vec_new.at[0], dst_ref=vec_w.at[me], send_sem=vec_send.at[k - 1, 1], recv_sem=vec_recv.at[k - 1, 1],
+            device_id=(lax.rem(me + k, n_dev),), device_id_type=MESH)
 
     def send_sib(t):
         for j in range(4):
             sib_copy(j, t).start()
 
-    def fetch(t):
+    def fetch(t, which):
         slot = lax.rem(t, 2)
 
         @pl.when(t < steps)
         def _():
-            for j in range(3):
-                sib_copy(j, t).wait_recv()
-            for piece in ('diag', 'x_b', 'y_a'):
-                for copy in raw_copies(piece, t, slot):
-                    copy.start()
+            for j, piece in enumerate(('diag', 'x_b', 'y_a')):
+                if which == 1:
+                    sib_copy(j, t).wait_recv()
+                raw_copy(piece, t, slot, which).start()
 
         @pl.when(jnp.logical_and(t >= 1, t <= steps))
         def _():
             for piece in ('x_a', 'y_b'):
-                for copy in raw_copies(piece, t - 1, slot):
-                    copy.start()
+                raw_copy(piece, t - 1, slot, which).start()
 
         @pl.when(jnp.logical_and(t >= 2, t <= steps + 1))
         def _():
-            sib_copy(3, t - 2).wait_recv()
-            for copy in raw_copies('mine', t - 2, slot):
-                copy.start()
-
+            if which == 1:
+                sib_copy(3, t - 2).wait_recv()
+            raw_copy('mine', t - 2, slot, which).start()
+
+    barrier = pltpu.get_barrier_semaphore()
+    for k in range(1, n_dev):
+        pl.semaphore_signal(barrier, inc=1, device_id=(lax.rem(me + k, n_dev),), device_id_type=MESH)
+    fetch(jnp.int32(0), 0)
+    pl.semaphore_wait(barrier, n_dev - 1)
     send_sib(0)
     send_sib(1)
     acc[...] = jnp.zeros_like(acc)
-    fetch(0)
+    fetch(jnp.int32(0), 1)
 
     @pl.loop(0, steps + 2)
     def _(t):
@@ -185,7 +184,8 @@
         def _():
             send_sib(t + 2)
 
-        fetch(t + 1)
+        fetch(t + 1, 0)
+        fetch(t + 1, 1)
 
         @pl.when(t < steps)
         def _():
@@ -208,8 +208,7 @@
         @pl.when(t == 0)
         def _():
             for k in range(1, n_dev):
-                for copy in vec_copies(k):
-                    copy.start()
+                row_copy(k).start()
 
         @pl.when(jnp.logical_and(t >= 1, t <= steps))
         def _():
@@ -253,6 +252,9 @@
                 acc[...] += jnp.sum((whole * whole).reshape(blk_rows // 8, 8, LANES), axis=0)
             out_copy(t - 2, slot).start()
 
+    for t in (steps - 2, steps - 1):
+        out_copy(t, t % 2).wait()
+
     def square_copy(k):
         target = lax.rem(me + k, n_dev)
         return pltpu.make_async_remote_copy(
@@ -262,26 +264,158 @@
     for k in range(1, n_dev):
         square_copy(k).start()
     sq_land[me] = acc[...]
-
-    own = [pltpu.make_async_copy(src, vec_land.at[me] if i == 0 else vec_state.at[i - 1, me], local_sem.at[i])
-           for i, src in enumerate(vec_srcs)]
-    for copy in own:
+    own_row = pltpu.make_async_copy(gv, vec_land.at[me], local_sem)
+    own_row.start()
+
+    share_rows = share // LANES
+    half_rows = share_rows // 2
+    w_rows = half_rows // w_steps
+
+    def inside(part, t, n=1):
+        return pl.ds(pl.multiple_of(part * half_rows + t * w_rows, 16), n * w_rows)
+
+    def place(dev, part, t):
+        return pl.ds(pl.multiple_of(dev * share_rows + part * half_rows + t * w_rows, 16), w_rows)
+
+    def state_copies(t, slot):
+        return [pltpu.make_async_copy(src.at[inside(part, t), :], state_in.at[slot, i, part], state_sem.at[slot, i, part])
+                for i, src in enumerate((total, p_mat, m_mat, s_mat)) for part in range(2)]
+
+    def own_copy(to, part, t):
+        target = (x_dev, y_dev, sib)[to]
+        recv = own_sib_recv if to == 2 else own_recv.at[to, part, t]
+        return pltpu.make_async_remote_copy(
+            src_ref=own_w.at[inside(part, t), :], dst_ref=gathered.at[place(me, part, t), :],
+            send_sem=own_send.at[to], recv_sem=recv, device_id=(target,), device_id_type=MESH)
+
+    def keep_copy(part, t):
+        return pltpu.make_async_copy(own_w.at[inside(part, t), :], gathered.at[place(me, part, t), :], keep_sem)
+
+    def late_copy(part):
+        return pltpu.make_async_copy(own_w.at[inside(part, w_steps - w_late, w_late), :], (late_a, late_b)[part],
+                                     late_sem.at[part])
+
+    def forward(part, t):
+        rows_at = place((x_dev, y_dev)[part], part, t)
+        return pltpu.make_async_remote_copy(
+            src_ref=gathered.at[rows_at, :], dst_ref=gathered.at[rows_at, :],
+            send_sem=fwd_send.at[part], recv_sem=fwd_recv.at[part, t],
+            device_id=((y_dev, x_dev)[part],), device_id_type=MESH)
+
+    def to_sib(dev, part, t):
+        rows_at = place(dev, part, t)
+        return pltpu.make_async_remote_copy(
+            src_ref=gathered.at[rows_at, :], dst_ref=gathered.at[rows_at, :],
+            send_sem=fsib_send, recv_sem=fsib_recv, device_id=(sib,), device_id_type=MESH)
+
+    def all_rows(n, send, recv):
+        return pltpu.make_async_remote_copy(
+            src_ref=gathered.at[pl.ds(0, n * w_rows), :], dst_ref=gathered.at[pl.ds(0, n * w_rows), :],
+            send_sem=send, recv_sem=recv, device_id=(sib,), device_id_type=MESH)
+
+    for copy in state_copies(0, 0):
         copy.start()
-    for copy in own:
-        copy.wait()
+
+    own_row.wait()
     for k in range(1, n_dev):
-        for copy in vec_copies(k):
-            copy.wait()
-    vec_rows = vec_out.shape[0]
+        row_copy(k).wait()
     vec_total = vec_land[0].astype(jnp.float32)
     for d in range(1, n_dev):
         vec_total += vec_land[d].astype(jnp.float32)
+    vec_rows = gv.shape[1] // LANES
     vec_total = vec_total.reshape(vec_rows, LANES)
-    vec_out[...] = vec_total
-    vec_square = jnp.sum((vec_total * vec_total).reshape(vec_rows // 8, 8, LANES), axis=0)
+    square = jnp.sum((vec_total * vec_total).reshape(vec_rows // 8, 8, LANES), axis=0)
+    own_rows = pv.shape[0]
+    mine = pl.ds(pl.multiple_of(me * own_rows * LANES, LANES), own_rows * LANES)
+    vec_sum = vec_land[0, :, mine].astype(jnp.float32)
+    for d in range(1, n_dev):
+        vec_sum += vec_land[d, :, mine].astype(jnp.float32)
+    vec_sum = vec_sum.reshape(own_rows, LANES)
+    for k in range(1, n_dev):
+        square_copy(k).wait()
+    for d in range(n_dev):
+        square += sq_land[d]
+    norm = jnp.sqrt(jnp.sum(jnp.sum(square, axis=0, keepdims=True), axis=1, keepdims=True))
+    coef = jnp.minimum(1.0, 1.0 / (norm + NORM_EPS))
+    coef_out[...] = jnp.broadcast_to(coef, coef_out.shape)
+
+    w_tiles = w_rows // 16
+    w_blk = 16 * max(d for d in range(1, 9) if w_tiles % d == 0)
+
+    def update(slot, part, t):
+        @pl.loop(0, w_rows // w_blk)
+        def _(i):
+            at = pl.ds(pl.multiple_of(i * w_blk, 16), w_blk)
+            grad, master, moment, second = (state_in[slot, k, part, at, :] for k in range(4))
+            new = adam_update(grad, coef_out[0:1, :], master, moment, second, DECAY)[0]
+            out = pl.ds(pl.multiple_of(part * half_rows + t * w_rows + i * w_blk, 16), w_blk)
+            own_w[out, :] = new.astype(jnp.bfloat16)
+
+    early = w_steps - w_late
+
+    @pl.loop(0, w_steps + LAG + 2)
+    def _(u):
+        slot = lax.rem(u, 2)
+
+        @pl.when(u + 1 < w_steps)
+        def _():
+            for copy in state_copies(u + 1, 1 - slot):
+                copy.start()
+
+        @pl.when(u < w_steps)
+        def _():
+            for copy in state_copies(u, slot):
+                copy.wait()
+            for part in range(2):
+                update(slot, part, u)
+                own_copy(part, part, u).start()
+
+                @pl.when(u < early)
+                def _():
+                    own_copy(1 - part, part, u).start()
+                own_copy(2, part, u).start()
+                keep_copy(part, u).start()
+
+        @pl.when(jnp.logical_and(u >= LAG, u < w_steps + LAG))
+        def _():
+            t = u - LAG
+            for part in range(2):
+                own_copy(part, part, t).wait_recv()
+                forward(part, t).start()
+                to_sib((x_dev, y_dev)[part], part, t).start()
+
+            @pl.when(t < early)
+            def _():
+                for part in range(2):
+                    own_copy(1 - part, part, t).wait_recv()
+                    to_sib((y_dev, x_dev)[part], part, t).start()
+
+        @pl.when(u >= LAG + 2)
+        def _():
+            t = u - LAG - 2
+            for part in range(2):
+                forward(part, t).wait_recv()
+                to_sib(g_dev, part, t).start()
+
+        @pl.when(u == 1)
+        def _():
+            new = adam_update(vec_sum, coef_out[0:1, :], pv[...], mv[...], sv[...], 0.0)
+            for i in range(3):
+                vec_new[i] = new[i]
+            vec_w[me] = new[0]
+            for k in range(1, n_dev):
+                new_copy(k).start()
+
+        @pl.when(u == w_steps - 1)
+        def _():
+            for part in range(2):
+                late_copy(part).start()
+
+    for k in range(1, n_dev):
+        new_copy(k).wait()
+
     for t in (steps - 2, steps - 1):
         slot = t % 2
-        out_copy(t, slot).wait()
         for part in range(2):
             leaf_copy(t, slot, part).wait_send()
             direct_copy(t, slot, part).wait_send()
@@ -289,36 +423,40 @@
     pltpu.make_async_remote_copy(
         src_ref=g.at[:, pl.ds(0, 4 * share)], dst_ref=sib_land, send_sem=sib_send, recv_sem=sib_recv.at[0, 0],
         device_id=(sib,), device_id_type=MESH).wait_send()
-    for k in range(1, n_dev):
-        square_copy(k).wait()
-    square = sq_land[0]
-    for d in range(1, n_dev):
-        square += sq_land[d]
-    square_out[...] = square + vec_square
-
-
-def reduce_call(g, gv, pv, mv, sv, share, steps):
+    for part in range(2):
+        late_copy(part).wait()
+        all_rows(w_steps + early, own_send.at[part], fsib_recv).wait_send()
+        all_rows(w_steps, fwd_send.at[part], fsib_recv).wait_send()
+    all_rows(2 * w_steps, own_send.at[2], own_sib_recv).wait()
+    all_rows(4 * w_steps + 2 * early, fsib_send, fsib_recv).wait()
+    pltpu.make_async_copy(own_w, gathered.at[pl.ds(0, share_rows), :], keep_sem).wait()
+
+
+def step_call(g, gv, p_mat, m_mat, s_mat, pv, mv, sv, share, steps, w_steps, w_late):
     half = share // (2 * steps)
     rows = half // LANES
     share_rows = share // LANES
+    w_rows = share_rows // (2 * w_steps)
     dma = pltpu.SemaphoreType.DMA
     f32, bf16 = jnp.float32, jnp.bfloat16
-    vec_rows = gv.shape[1] // LANES
     own_rows = pv.shape[0]
-    any_spec = pl.BlockSpec(memory_space=pltpu.HBM)
+    hbm = pl.BlockSpec(memory_space=pltpu.HBM)
     vmem = pl.BlockSpec(memory_space=pltpu.VMEM)
     return pl.pallas_call(
-        functools.partial(reduce_kernel, share, half, steps),
+        functools.partial(step_kernel, share, half, steps, w_steps, w_late),
         out_shape=(jax.ShapeDtypeStruct((share_rows, LANES), f32),
+                   jax.ShapeDtypeStruct((8 * share_rows, LANES), bf16),
+                   jax.ShapeDtypeStruct((w_late * w_rows, LANES), bf16),
+                   jax.ShapeDtypeStruct((w_late * w_rows, LANES), bf16),
                    jax.ShapeDtypeStruct((1, 4 * share), bf16),
                    jax.ShapeDtypeStruct((share_rows, LANES), f32),
                    jax.ShapeDtypeStruct((share_rows, LANES), f32),
                    jax.ShapeDtypeStruct((share_rows, LANES), f32),
                    jax.ShapeDtypeStruct((8, LANES), f32),
-                   jax.ShapeDtypeStruct((vec_rows, LANES), f32),
-                   jax.ShapeDtypeStruct((3, 8, own_rows, LANES), f32)),
-        in_specs=[any_spec] + [vmem] * 4,
-        out_specs=(any_spec,) * 5 + (vmem,) * 3,
+                   jax.ShapeDtypeStruct((3, own_rows, LANES), f32),
+                   jax.ShapeDtypeStruct((8, own_rows, LANES), f32)),
+        in_specs=[hbm, vmem, hbm, hbm, hbm, vmem, vmem, vmem],
+        out_specs=(hbm,) * 8 + (vmem,) * 3,
         scratch_shapes=[
             pltpu.VMEM((2, 1, 8 * half), bf16),
             pltpu.VMEM((2, 1, 8 * half), bf16),
@@ -334,31 +472,177 @@
             dma(()), dma((4, steps)),
             dma((2, 2)), dma((2, steps)), dma((2, 2)), dma((2, steps)), dma((2, 2)), dma((2, steps)),
             dma((2, 6)), dma((2, 6)), dma((2,)), dma((2,)), dma((2,)),
-            dma((7,)), dma((7,)), dma((7, 4)), dma((7, 4)), dma((4,)),
+            dma((7,)), dma((7,)), dma((7, 2)), dma((7, 2)), dma(()),
+            pltpu.VMEM((2, 4, 2, w_rows, LANES), f32),
+            pltpu.VMEM((share_rows, LANES), bf16),
+            dma((2, 4, 2)), dma((3,)), dma((2, 2, w_steps)), dma(()), dma(()), dma((2,)),
+            dma((2,)), dma((2, w_steps)), dma(()), dma(()),
         ],
         compiler_params=pltpu.CompilerParams(collective_id=0, has_side_effects=True, vmem_limit_bytes=60 * 2**20),
-        name='reduce_share',
-    )(g, gv, pv, mv, sv)
-
-
-STEPS = 14
+        name='reduce_update_gather',
+    )(g, gv, p_mat, m_mat, s_mat, pv, mv, sv)
+
+
+def update_kernel(coef, grad, master, moment, second, vec_new, vec_w, new_p, new_m, new_s, vec_p, vec_m, vec_s, w_vec,
+                  rows):
+    new_p[...], new_m[...], new_s[...] = adam_update(grad[...], coef[0:1, :], master[...], moment[...], second[...], DECAY)
+
+    @pl.when(pl.program_id(0) == 0)
+    def _():
+        vec_p[...], vec_m[...], vec_s[...] = vec_new[0], vec_new[1], vec_new[2]
+        n = vec_w.shape[1]
+        for d in range(vec_w.shape[0]):
+            rows[pl.ds(d * n, n), :] = vec_w[d]
+        w_vec[...] = rows[...].astype(jnp.bfloat16)
+
+
+def update_call(coef, grad, master, moment, second, vec_new, vec_w, block):
+    n = grad.shape[0]
+    own_rows = vec_new.shape[1]
+    f32 = jnp.float32
+    tile = pl.BlockSpec((block, LANES), lambda i: (i, 0))
+
+    def whole(shape):
+        return pl.BlockSpec(shape, lambda i: (0,) * len(shape))
+
+    small = jax.ShapeDtypeStruct((own_rows, LANES), f32)
+    return pl.pallas_call(
+        update_kernel,
+        grid=(n // block,),
+        out_shape=(jax.ShapeDtypeStruct(grad.shape, f32),) * 3 + (small,) * 3 + (
+            jax.ShapeDtypeStruct((8 * own_rows, LANES), jnp.bfloat16),),
+        in_specs=[whole((8, LANES))] + [tile] * 4 + [whole(vec_new.shape), whole(vec_w.shape)],
+        out_specs=(tile,) * 3 + (whole((own_rows, LANES)),) * 3 + (whole((8 * own_rows, LANES)),),
+        scratch_shapes=[pltpu.VMEM((8 * own_rows, LANES), f32)],
+        compiler_params=pltpu.CompilerParams(vmem_limit_bytes=40 * 2**20),
+        cost_estimate=pl.CostEstimate(flops=n * LANES * 200, bytes_accessed=n * LANES * 28, transcendentals=0),
+        name='update',
+    )(coef, grad, master, moment, second, vec_new, vec_w)
+
+
+def copy_kernel(moves, blocks, *refs):
+    n_src = 1 + max(move[0] for move in moves(0))
+    srcs, out, buf, in_sem, out_sem = refs[:n_src], refs[-4], refs[-3], refs[-2], refs[-1]
+    me = lax.axis_index('fsdp')
+    todo = []
+    for which, src_row, dst_row, n in moves(me):
+        size = n // blocks(n)
+        for i in range(blocks(n)):
+            todo.append((srcs[which], src_row + i * size, dst_row + i * size, size))
+    slots = buf.shape[0]
+
+    def take(k):
+        src, src_row, _, size = todo[k]
+        return pltpu.make_async_copy(src.at[pl.ds(pl.multiple_of(src_row, 16), size), :],
+                                     buf.at[k % slots, pl.ds(0, size), :], in_sem.at[k % slots])
+
+    def give(k):
+        _, _, dst_row, size = todo[k]
+        return pltpu.make_async_copy(buf.at[k % slots, pl.ds(0, size), :],
+                                     out.at[pl.ds(pl.multiple_of(dst_row, 16), size), :], out_sem.at[k % slots])
+
+    ahead = slots // 2
+    for k in range(min(ahead, len(todo))):
+        take(k).start()
+    for k in range(len(todo)):
+        take(k).wait()
+        give(k).start()
+        if k + ahead < len(todo):
+            if k + ahead >= slots:
+                give(k + ahead - slots).wait()
+            take(k + ahead).start()
+    for k in range(max(0, len(todo) - slots), len(todo)):
+        give(k).wait()
+
+
+def copy_call(name, moves, srcs, out_rows, into=None, slots=12, most=4160):
+    def blocks(n):
+        return next(d for d in range(1, n // 16 + 1) if (n // 16) % d == 0 and n // d <= most)
+
+    hbm = pl.BlockSpec(memory_space=pltpu.HBM)
+    args = list(srcs) + ([into] if into is not None else [])
+    size = sum(move[3] for move in moves(0)) * LANES * 2
+    return pl.pallas_call(
+        functools.partial(copy_kernel, moves, blocks),
+        out_shape=jax.ShapeDtypeStruct((out_rows, LANES), jnp.bfloat16),
+        in_specs=[hbm] * len(args),
+        out_specs=hbm,
+        scratch_shapes=[pltpu.VMEM((slots, most, LANES), jnp.bfloat16),
+                        pltpu.SemaphoreType.DMA((slots,)), pltpu.SemaphoreType.DMA((slots,))],
+        input_output_aliases={len(srcs): 0} if into is not None else {},
+        compiler_params=pltpu.CompilerParams(vmem_limit_bytes=32 * 2**20),
+        cost_estimate=pl.CostEstimate(flops=size * 6, bytes_accessed=2 * size, transcendentals=0),
+        name=name,
+    )(*args)
+
+
+def block_rows_of(n):
+    return 16 * max(d for d in range(1, 190) if (n // 16) % d == 0)
+
+
+STEPS = 28
+W_STEPS = 14
+W_LATE = 10
+LAG = 3
+
+
+def neighbours(me):
+    core, x_pos, y_pos = lax.rem(me, 2), lax.rem(me // 2, 2), me // 4
+    return me + 1 - 2 * core, me + 2 - 4 * x_pos, me + 4 - 8 * y_pos
 
 
 def solution(mesh):
+    hop_x = [(d, d ^ 2) for d in range(8)]
+    hop_y = [(d, d ^ 4) for d in range(8)]
+    hop_core = [(d, d ^ 1) for d in range(8)]
+
     def local_step(grad_mat, grad_vec, master_mat, moment_mat, second_mat, master_vec, moment_vec, second_vec):
         share = master_mat.shape[0]
+        share_rows = share // LANES
+        half_rows = share_rows // 2
+        late = W_LATE * (half_rows // W_STEPS)
+        early = half_rows - late
         own_rows = master_vec.shape[0] // LANES
+        mats = [v.reshape(share_rows, LANES) for v in (master_mat, moment_mat, second_mat)]
         vecs = [v.reshape(own_rows, LANES) for v in (master_vec, moment_vec, second_vec)]
-        total, _, _, _, _, square, vec_sum, vec_state = reduce_call(grad_mat, grad_vec, *vecs, share, STEPS)
-        total_norm = jnp.sqrt(jnp.sum(square))
-        clip_coef = jnp.minimum(1.0, 1.0 / (total_norm + NORM_EPS))
-        new_mat = adam_update(total.reshape(-1), clip_coef, master_mat, moment_mat, second_mat, DECAY)
-        weights_mat = lax.all_gather(new_mat[0].astype(jnp.bfloat16), 'fsdp', tiled=True)
-        vec_state = vec_state.reshape(3, -1)
-        vec_new = adam_update(vec_sum.reshape(-1), clip_coef, vec_state[0], vec_state[1], vec_state[2], 0.0)
-        at = lax.axis_index('fsdp') * master_vec.shape[0]
-        new_vec = tuple(lax.dynamic_slice(v, (at,), master_vec.shape) for v in vec_new)
-        return new_mat + new_vec + (weights_mat, vec_new[0].astype(jnp.bfloat16))
+        total, gathered, late_a, late_b, _, _, _, _, coef, vec_new, vec_w = step_call(
+            grad_mat, grad_vec, *mats, *vecs, share, STEPS, W_STEPS, W_LATE)
+
+        from_x = lax.ppermute(late_b, 'fsdp', hop_x)
+        from_y = lax.ppermute(late_a, 'fsdp', hop_y)
+
+        def whole_moves(me):
+            sib, x_dev, y_dev = neighbours(me)
+            g_dev = x_dev + y_dev - me
+            flip = sib - me
+            return [(0, dev * share_rows, dev * share_rows, share_rows) for dev in (me, sib, g_dev, g_dev + flip)]
+
+        def early_moves(me):
+            sib, x_dev, y_dev = neighbours(me)
+            flip = sib - me
+            moves = []
+            for dev in (x_dev, x_dev + flip):
+                moves.append((0, dev * share_rows, dev * share_rows, half_rows + early))
+            for dev in (y_dev, y_dev + flip):
+                moves.append((0, dev * share_rows, dev * share_rows, early))
+                moves.append((0, dev * share_rows + half_rows, dev * share_rows + half_rows, half_rows))
+            return moves + [(1, 0, x_dev * share_rows + half_rows + early, late),
+                            (2, 0, y_dev * share_rows + early, late)]
+
+        def late_moves(me):
+            sib, x_dev, y_dev = neighbours(me)
+            flip = sib - me
+            return [(0, 0, (x_dev + flip) * share_rows + half_rows + early, late),
+                    (1, 0, (y_dev + flip) * share_rows + early, late)]
+
+        *new, weights_vec = update_call(coef, total, *mats, vec_new, vec_w, block_rows_of(share_rows))
+        weights = copy_call('collect_whole', whole_moves, (gathered,), 8 * share_rows)
+        from_x, from_y, weights, *new = lax.optimization_barrier((from_x, from_y, weights, *new))
+        sib_x = lax.ppermute(from_x, 'fsdp', hop_core)
+        sib_y = lax.ppermute(from_y, 'fsdp', hop_core)
+        weights = copy_call('collect_early', early_moves, (gathered, from_x, from_y), 8 * share_rows, into=weights)
+        weights = copy_call('collect_late', late_moves, (sib_x, sib_y), 8 * share_rows, into=weights)
+        return tuple(v.reshape(-1) for v in (*new, weights, weights_vec))
 
     row_spec = P('fsdp', None)
     flat_spec = P('fsdp')

time: 871 us -> 774 us (0.89)
  waiting for transfers between devices: 263 us -> 0.52 us
  Pallas kernels: 509 us -> 769 us
  local copies, waits for them, and re-layouts: 41.6 us -> 0.01 us
  other arithmetic: 40.7 us -> 0 us
  between operations: 14.8 us -> 0.7 us
    all_gather x1 -> x0, waiting for transfers between devices: 263 us -> none  [local_step(): lax.all_gather(new_mat[0].astype(jnp.bfloat16), 'fsdp', tiled=True)]
    pallas_call x1 -> x5, Pallas kernels: 509 us -> 769 us  [the longest x1 692 us: step_call(): pl.pallas_call(functools.partial(step_kernel, share, half, steps, w_steps...]
    unnamed x5 -> x6, local copies, waits for them, and re-layouts: 39.6 us -> 0.01 us
    convert_element_type x2 -> x0, other arithmetic: 39.4 us -> none  [the longest x1 38.8 us: local_step(): new_mat[0].astype(jnp.bfloat16)]
  transfers between devices with their start and end apart: 1 -> 4, of which waited for: 1 -> 2; matrix products, arithmetic and copies ran while one was open for 0% -> 0% of each run, Pallas kernels for 0% -> 9%
where the time goes in v2:
time: 774 us; the launch traced here: 772 us
  Pallas kernels  769 us (99%)
    pallas_call x1, Pallas kernels, step_call(): pl.pallas_call(functools.partial(step_kernel, share, half, steps, w_steps...  692 us
    pallas_call x3, Pallas kernels, copy_call(): pl.pallas_call(functools.partial(copy_kernel, moves, blocks), out_shape=j...  38.7 us
    pallas_call x1, Pallas kernels, update_call(): pl.pallas_call(update_kernel, grid=(n // block,), out_shape=(jax.ShapeDty...  37.5 us
  transfers between devices with their start and end apart: 4, of which 2 were waited for; matrix products, arithmetic and copies ran while one was open for 0% of the time, Pallas kernels for 9%

profile of v2, /device:TPU:0, one launch (start us, length us, event | category | flops | bytes accessed | tf_op | source)
XLA Modules:
  0.0 772.3 jit_solution(13384851836689865766)
XLA Ops:
  0.6 692.4 %reduce_update_gather.1 = (f32[29120,128]{1,0:T(8,128)}, bf16[232960,128]{1,0:T(8,128)(2,1)}, bf16[10400,128]{1,0:T(8,128)(2,1)}, bf16[10400,128]{1,0:T(8,128)(2...) custom-call(bf16[1,29818880]{1,0:T(2,128)(2,1)} %g.1, ...), custom_call_target="tpu_custom_call" | custom-call | tf_op jit(solution)/shard_map/reduce_update_gather/pallas_call | solution.py:445
  693.1 0.7 collective-permute-start
  693.7 1.3 collective-permute-start.1
  695.1 0.0 copy-start
  695.1 0.0 copy-start.1
  695.1 0.0 copy-start.2
  695.1 20.3 %collect_whole.1.refs_3_ = bf16[232960,128]{1,0:T(8,128)(2,1)} custom-call(bf16[232960,128]{1,0:T(8,128)(2,1)} %get-tuple-element.33.refs_0_), custom_call_target="tpu_custom_call" | custom-call | flops 178913280 | bytes 59637760 | tf_op jit(solution)/shard_map/collect_whole/pallas_call | solution.py:565
  715.4 0.0 copy-done
  715.4 0.0 copy-done.1
  715.4 0.0 copy-done.2
  715.4 37.5 %update.1 = (f32[29120,128]{1,0:T(8,128)}, f32[29120,128]{1,0:T(8,128)}, f32[29120,128]{1,0:T(8,128)}, f32[6,128]{1,0:T(8,128)}, f32[6,128]{1,0:T(8,128)}, /*index=5*/f32[6,128]{1,0:T(8,128)}, bf16[48,128]{1,0:T(8,128)(2,1)}) custom-call(f32[8,128]{1,0:T(8,128)S(1)} %copy-done.2, f32[29120,128]{1,0:T(8,128)} %get-tuple-element.35.grad, ...), custom_call_target="tpu_custom_call" | custom-call | flops 745472000 | bytes 104366080 | tf_op jit(solution)/shard_map/update/pallas_call | solution.py:509
  752.9 0.2 collective-permute-done.refs_1_
  753.1 0.4 collective-permute-done.1.refs_2_
  753.4 0.0 collective-permute-start.2
  753.4 0.5 collective-permute-start.3
  753.9 15.5 %collect_early.1.refs_2_ = bf16[232960,128]{1,0:T(8,128)(2,1)} custom-call(bf16[232960,128]{1,0:T(8,128)(2,1)} %get-tuple-element.33.refs_0_, bf16[10400,128]{1,0:T(8,128)(2,1)S(1)} %collective-permute-done.refs_1_, bf16[10400,128]{1,0:T(8,128)(2,1)S(1)} %collective-permute-done.1.refs_2_, ...), custom_call_target="tpu_custom_call", output_to_operand_aliasing={{}: (3, {})} | custom-call | flops 146964480 | bytes 48988160 | tf_op jit(solution)/shard_map/collect_early/pallas_call | solution.py:565
  769.4 0.0 collective-permute-done.2.refs_0_
  769.4 0.0 collective-permute-done.3.refs_1_
  769.5 2.9 collect_late.1
Async XLA Ops:
  693.1 60.0 %collective-permute-start = (bf16[10400,128]{1,0:T(8,128)(2,1)}, bf16[10400,128]{1,0:T(8,128)(2,1)S(1)}, u32[]{:S(2)}, u32[]{:S(2)}) collective-permute-start(bf16[10400,128]{1,0:T(8,128)(2,1)} %get-tuple-element.31), channel_id=1, source_target_pairs={{0,2},{1,3},{2,0},{3,1},{4,6},{5,7},{6,4},{7,5}} | collective-permute-start | bytes 7987208 | tf_op jit(solution)/shard_map/ppermute | solution.py:611
  693.7 59.7 %collective-permute-start.1 = (bf16[10400,128]{1,0:T(8,128)(2,1)}, bf16[10400,128]{1,0:T(8,128)(2,1)S(1)}, u32[]{:S(2)}, u32[]{:S(2)}) collective-permute-start(bf16[10400,128]{1,0:T(8,128)(2,1)} %get-tuple-element.32), channel_id=1, source_target_pairs={{0,4},{1,5},{2,6},{3,7},{4,0},{5,1},{6,2},{7,3}} | collective-permute-start | bytes 7987208 | tf_op jit(solution)/shard_map/ppermute | solution.py:612
  695.1 20.3 %copy-start = (f32[8,6,128]{2,1,0:T(8,128)S(1)}, f32[8,6,128]{2,1,0:T(8,128)}, u32[]{:S(2)}) copy-start(f32[8,6,128]{2,1,0:T(8,128)} %get-tuple-element.37.vec_w) | copy-start | bytes 73732
  695.1 20.3 %copy-start.1 = (f32[3,6,128]{2,1,0:T(8,128)S(1)}, f32[3,6,128]{2,1,0:T(8,128)}, u32[]{:S(2)}) copy-start(f32[3,6,128]{2,1,0:T(8,128)} %get-tuple-element.36.vec_new) | copy-start | bytes 27652
  695.1 20.3 %copy-start.2 = (f32[8,128]{1,0:T(8,128)S(1)}, f32[8,128]{1,0:T(8,128)}, u32[]{:S(2)}) copy-start(f32[8,128]{1,0:T(8,128)} %get-tuple-element.34.coef) | copy-start | bytes 12292
  753.4 16.0 %collective-permute-start.2 = (bf16[10400,128]{1,0:T(8,128)(2,1)S(1)}, bf16[10400,128]{1,0:T(8,128)(2,1)S(1)}, u32[]{:S(2)}, u32[]{:S(2)}) collective-permute-start(bf16[10400,128]{1,0:T(8,128)(2,1)S(1)} %collective-permute-done.refs_1_), channel_id=1, source_target_pairs={{0,1},{1,0},{2,3},{3,2},{4,5},{5,4},{6,7},{7,6}} | collective-permute-start | bytes 7987208 | tf_op jit(solution)/shard_map/ppermute | solution.py:641
  753.4 16.0 %collective-permute-start.3 = (bf16[10400,128]{1,0:T(8,128)(2,1)S(1)}, bf16[10400,128]{1,0:T(8,128)(2,1)S(1)}, u32[]{:S(2)}, u32[]{:S(2)}) collective-permute-start(bf16[10400,128]{1,0:T(8,128)(2,1)S(1)} %collective-permute-done.1.refs_2_), channel_id=1, source_target_pairs={{0,1},{1,0},{2,3},{3,2},{4,5},{5,4},{6,7},{7,6}} | collective-permute-start | bytes 7987208 | tf_op jit(solution)/shard_map/ppermute | solution.py:642

commit v3 on v2

--- a/solution.py
+++ b/solution.py
@@ -40,7 +40,7 @@
 
 
 def step_kernel(share, half, steps, w_steps, w_late, g, gv, p_mat, m_mat, s_mat, pv, mv, sv,
-                total, gathered, late_a, late_b, sib_land, leaf_land, four_land, direct_land, coef_out, vec_new, vec_w,
+                total, gathered, late_a, late_b, last_a, last_b, sib_land, leaf_land, four_land, direct_land, coef_out, vec_new, vec_w,
                 raw_own, raw_sib, leaf_st, direct_st, four_st, leaf_in, fin_in, out_st, acc, sq_land, vec_land,
                   sib_send, sib_recv, leaf_send, leaf_recv, four_send, four_recv, direct_send, direct_recv,
                   own_sem, sibin_sem, leafin_sem, fin_sem, out_sem, sq_send, sq_recv, vec_send, vec_recv, local_sem,
@@ -252,9 +252,6 @@
                 acc[...] += jnp.sum((whole * whole).reshape(blk_rows // 8, 8, LANES), axis=0)
             out_copy(t - 2, slot).start()
 
-    for t in (steps - 2, steps - 1):
-        out_copy(t, t % 2).wait()
-
     def square_copy(k):
         target = lax.rem(me + k, n_dev)
         return pltpu.make_async_remote_copy(
@@ -264,6 +261,8 @@
     for k in range(1, n_dev):
         square_copy(k).start()
     sq_land[me] = acc[...]
+    for t in (steps - 2, steps - 1):
+        out_copy(t, t % 2).wait()
     own_row = pltpu.make_async_copy(gv, vec_land.at[me], local_sem)
     own_row.start()
 
@@ -291,9 +290,10 @@
     def keep_copy(part, t):
         return pltpu.make_async_copy(own_w.at[inside(part, t), :], gathered.at[place(me, part, t), :], keep_sem)
 
-    def late_copy(part):
-        return pltpu.make_async_copy(own_w.at[inside(part, w_steps - w_late, w_late), :], (late_a, late_b)[part],
-                                     late_sem.at[part])
+    def late_copy(group, part):
+        start = w_steps - sum(w_late[group:])
+        return pltpu.make_async_copy(own_w.at[inside(part, start, w_late[group]), :],
+                                     ((late_a, late_b), (last_a, last_b))[group][part], late_sem.at[group, part])
 
     def forward(part, t):
         rows_at = place((x_dev, y_dev)[part], part, t)
@@ -351,7 +351,7 @@
             out = pl.ds(pl.multiple_of(part * half_rows + t * w_rows + i * w_blk, 16), w_blk)
             own_w[out, :] = new.astype(jnp.bfloat16)
 
-    early = w_steps - w_late
+    early = w_steps - sum(w_late)
 
     @pl.loop(0, w_steps + LAG + 2)
     def _(u):
@@ -408,8 +408,9 @@
 
         @pl.when(u == w_steps - 1)
         def _():
-            for part in range(2):
-                late_copy(part).start()
+            for group in range(2):
+                for part in range(2):
+                    late_copy(group, part).start()
 
     for k in range(1, n_dev):
         new_copy(k).wait()
@@ -424,7 +425,8 @@
         src_ref=g.at[:, pl.ds(0, 4 * share)], dst_ref=sib_land, send_sem=sib_send, recv_sem=sib_recv.at[0, 0],
         device_id=(sib,), device_id_type=MESH).wait_send()
     for part in range(2):
-        late_copy(part).wait()
+        late_copy(0, part).wait()
+        late_copy(1, part).wait()
         all_rows(w_steps + early, own_send.at[part], fsib_recv).wait_send()
         all_rows(w_steps, fwd_send.at[part], fsib_recv).wait_send()
     all_rows(2 * w_steps, own_send.at[2], own_sib_recv).wait()
@@ -446,8 +448,10 @@
         functools.partial(step_kernel, share, half, steps, w_steps, w_late),
         out_shape=(jax.ShapeDtypeStruct((share_rows, LANES), f32),
                    jax.ShapeDtypeStruct((8 * share_rows, LANES), bf16),
-                   jax.ShapeDtypeStruct((w_late * w_rows, LANES), bf16),
-                   jax.ShapeDtypeStruct((w_late * w_rows, LANES), bf16),
+                   jax.ShapeDtypeStruct((w_late[0] * w_rows, LANES), bf16),
+                   jax.ShapeDtypeStruct((w_late[0] * w_rows, LANES), bf16),
+                   jax.ShapeDtypeStruct((w_late[1] * w_rows, LANES), bf16),
+                   jax.ShapeDtypeStruct((w_late[1] * w_rows, LANES), bf16),
                    jax.ShapeDtypeStruct((1, 4 * share), bf16),
                    jax.ShapeDtypeStruct((share_rows, LANES), f32),
                    jax.ShapeDtypeStruct((share_rows, LANES), f32),
@@ -456,7 +460,7 @@
                    jax.ShapeDtypeStruct((3, own_rows, LANES), f32),
                    jax.ShapeDtypeStruct((8, own_rows, LANES), f32)),
         in_specs=[hbm, vmem, hbm, hbm, hbm, vmem, vmem, vmem],
-        out_specs=(hbm,) * 8 + (vmem,) * 3,
+        out_specs=(hbm,) * 10 + (vmem,) * 3,
         scratch_shapes=[
             pltpu.VMEM((2, 1, 8 * half), bf16),
             pltpu.VMEM((2, 1, 8 * half), bf16),
@@ -475,7 +479,7 @@
             dma((7,)), dma((7,)), dma((7, 2)), dma((7, 2)), dma(()),
             pltpu.VMEM((2, 4, 2, w_rows, LANES), f32),
             pltpu.VMEM((share_rows, LANES), bf16),
-            dma((2, 4, 2)), dma((3,)), dma((2, 2, w_steps)), dma(()), dma(()), dma((2,)),
+            dma((2, 4, 2)), dma((3,)), dma((2, 2, w_steps)), dma(()), dma(()), dma((2, 2)),
             dma((2,)), dma((2, w_steps)), dma(()), dma(()),
         ],
         compiler_params=pltpu.CompilerParams(collective_id=0, has_side_effects=True, vmem_limit_bytes=60 * 2**20),
@@ -582,7 +586,7 @@
 
 STEPS = 28
 W_STEPS = 14
-W_LATE = 10
+W_LATE = (10, 2)
 LAG = 3
 
 
@@ -600,16 +604,18 @@
         share = master_mat.shape[0]
         share_rows = share // LANES
         half_rows = share_rows // 2
-        late = W_LATE * (half_rows // W_STEPS)
-        early = half_rows - late
+        late, last = (n * (half_rows // W_STEPS) for n in W_LATE)
+        early = half_rows - late - last
         own_rows = master_vec.shape[0] // LANES
         mats = [v.reshape(share_rows, LANES) for v in (master_mat, moment_mat, second_mat)]
         vecs = [v.reshape(own_rows, LANES) for v in (master_vec, moment_vec, second_vec)]
-        total, gathered, late_a, late_b, _, _, _, _, coef, vec_new, vec_w = step_call(
+        total, gathered, late_a, late_b, last_a, last_b, _, _, _, _, coef, vec_new, vec_w = step_call(
             grad_mat, grad_vec, *mats, *vecs, share, STEPS, W_STEPS, W_LATE)
 
-        from_x = lax.ppermute(late_b, 'fsdp', hop_x)
-        from_y = lax.ppermute(late_a, 'fsdp', hop_y)
+        late_x = lax.ppermute(late_b, 'fsdp', hop_x)
+        late_y = lax.ppermute(late_a, 'fsdp', hop_y)
+        last_x = lax.ppermute(last_b, 'fsdp', hop_x)
+        last_y = lax.ppermute(last_a, 'fsdp', hop_y)
 
         def whole_moves(me):
             sib, x_dev, y_dev = neighbours(me)
@@ -626,22 +632,34 @@
             for dev in (y_dev, y_dev + flip):
                 moves.append((0, dev * share_rows, dev * share_rows, early))
                 moves.append((0, dev * share_rows + half_rows, dev * share_rows + half_rows, half_rows))
-            return moves + [(1, 0, x_dev * share_rows + half_rows + early, late),
-                            (2, 0, y_dev * share_rows + early, late)]
-
-        def late_moves(me):
+            return moves
+
+        def late_rows(x_dev, y_dev):
+            return [(0, 0, x_dev * share_rows + half_rows + early, late),
+                    (1, 0, y_dev * share_rows + early, late),
+                    (2, 0, x_dev * share_rows + half_rows + early + late, last),
+                    (3, 0, y_dev * share_rows + early + late, last)]
+
+        def own_late_moves(me):
+            _, x_dev, y_dev = neighbours(me)
+            return late_rows(x_dev, y_dev)
+
+        def sib_late_moves(me):
             sib, x_dev, y_dev = neighbours(me)
-            flip = sib - me
-            return [(0, 0, (x_dev + flip) * share_rows + half_rows + early, late),
-                    (1, 0, (y_dev + flip) * share_rows + early, late)]
+            return late_rows(x_dev + sib - me, y_dev + sib - me)
 
         *new, weights_vec = update_call(coef, total, *mats, vec_new, vec_w, block_rows_of(share_rows))
         weights = copy_call('collect_whole', whole_moves, (gathered,), 8 * share_rows)
-        from_x, from_y, weights, *new = lax.optimization_barrier((from_x, from_y, weights, *new))
-        sib_x = lax.ppermute(from_x, 'fsdp', hop_core)
-        sib_y = lax.ppermute(from_y, 'fsdp', hop_core)
-        weights = copy_call('collect_early', early_moves, (gathered, from_x, from_y), 8 * share_rows, into=weights)
-        weights = copy_call('collect_late', late_moves, (sib_x, sib_y), 8 * share_rows, into=weights)
+        late_x, late_y, weights, *new = lax.optimization_barrier((late_x, late_y, weights, *new))
+        sib_late_x = lax.ppermute(late_x, 'fsdp', hop_core)
+        sib_late_y = lax.ppermute(late_y, 'fsdp', hop_core)
+        weights = copy_call('collect_early', early_moves, (gathered,), 8 * share_rows, into=weights)
+        last_x, last_y, weights = lax.optimization_barrier((last_x, last_y, weights))
+        sib_last_x = lax.ppermute(last_x, 'fsdp', hop_core)
+        sib_last_y = lax.ppermute(last_y, 'fsdp', hop_core)
+        weights = copy_call('collect_late', own_late_moves, (late_x, late_y, last_x, last_y), 8 * share_rows, into=weights)
+        weights = copy_call('collect_last', sib_late_moves, (sib_late_x, sib_late_y, sib_last_x, sib_last_y),
+                            8 * share_rows, into=weights)
         return tuple(v.reshape(-1) for v in (*new, weights, weights_vec))
 
     row_spec = P('fsdp', None)

time: 774 us -> 766 us (0.990)
  Pallas kernels: 769 us -> 757 us
    pallas_call x1, Pallas kernels: 692 us -> 680 us  [step_call(): pl.pallas_call(functools.partial(step_kernel, share, half, steps, w_steps...]
    pallas_call x3 -> x4, Pallas kernels: 38.7 us -> 39 us  [copy_call(): pl.pallas_call(functools.partial(copy_kernel, moves, blocks), out_shape=j...]
  transfers between devices with their start and end apart: 4 -> 8, of which waited for: 2 -> 3; matrix products, arithmetic and copies ran while one was open for 0% -> 0% of each run, Pallas kernels for 9% -> 10%
where the time goes in v3:
time: 766 us; the launch traced here: 764 us
  Pallas kernels  757 us (99%)
    pallas_call x1, Pallas kernels, step_call(): pl.pallas_call(functools.partial(step_kernel, share, half, steps, w_steps...  680 us
    pallas_call x4, Pallas kernels, copy_call(): pl.pallas_call(functools.partial(copy_kernel, moves, blocks), out_shape=j...  39 us
    pallas_call x1, Pallas kernels, update_call(): pl.pallas_call(update_kernel, grid=(n // block,), out_shape=(jax.ShapeDty...  37.6 us
  transfers between devices with their start and end apart: 8, of which 3 were waited for; matrix products, arithmetic and copies ran while one was open for 0% of the time, Pallas kernels for 10%

profile of v3, /device:TPU:0, one launch (start us, length us, event | category | flops | bytes accessed | tf_op | source)
XLA Modules:
  0.0 763.8 jit_solution(12707538536574661827)
XLA Ops:
  0.6 680.2 %reduce_update_gather.1 = (f32[29120,128]{1,0:T(8,128)}, bf16[232960,128]{1,0:T(8,128)(2,1)}, bf16[10400,128]{1,0:T(8,128)(2,1)}, bf16[10400,128]{1,0:T(8,128)(2...) custom-call(bf16[1,29818880]{1,0:T(2,128)(2,1)} %g.1, ...), custom_call_target="tpu_custom_call" | custom-call | tf_op jit(solution)/shard_map/reduce_update_gather/pallas_call | solution.py:447
  680.9 0.7 collective-permute-start
  681.5 1.3 collective-permute-start.1
  682.9 0.0 copy-start
  682.9 0.0 copy-start.1
  682.9 0.0 copy-start.2
  682.9 20.3 %collect_whole.1.refs_1_ = bf16[232960,128]{1,0:T(8,128)(2,1)} custom-call(bf16[232960,128]{1,0:T(8,128)(2,1)} %get-tuple-element.38.refs_0_), custom_call_target="tpu_custom_call" | custom-call | flops 178913280 | bytes 59637760 | tf_op jit(solution)/shard_map/collect_whole/pallas_call | solution.py:569
  703.2 0.0 copy-done
  703.2 0.0 copy-done.1
  703.2 0.0 copy-done.2
  703.2 0.0 copy-start.4
  703.2 0.0 copy-start.3
  703.2 37.6 %update.1 = (f32[29120,128]{1,0:T(8,128)}, f32[29120,128]{1,0:T(8,128)}, f32[29120,128]{1,0:T(8,128)}, f32[6,128]{1,0:T(8,128)}, f32[6,128]{1,0:T(8,128)}, /*index=5*/f32[6,128]{1,0:T(8,128)}, bf16[48,128]{1,0:T(8,128)(2,1)}) custom-call(f32[8,128]{1,0:T(8,128)S(1)} %copy-done.2, f32[29120,128]{1,0:T(8,128)} %get-tuple-element.40.grad, ...), custom_call_target="tpu_custom_call" | custom-call | flops 745472000 | bytes 104366080 | tf_op jit(solution)/shard_map/update/pallas_call | solution.py:513
  740.8 0.1 collective-permute-done.refs_0_
  740.9 0.4 collective-permute-done.1.refs_1_
  741.2 0.0 collective-permute-start.2
  741.2 0.5 collective-permute-start.3
  741.7 0.0 copy-done.4
  741.7 1.4 collective-permute-start.4
  743.1 0.0 copy-done.3
  743.1 0.6 collective-permute-start.5
  743.8 12.3 %collect_early.1.refs_4_ = bf16[232960,128]{1,0:T(8,128)(2,1)} custom-call(bf16[232960,128]{1,0:T(8,128)(2,1)} %get-tuple-element.38.refs_0_, bf16[232960,128]{1,0:T(8,128)(2,1)} %collect_whole.1.refs_1_), custom_call_target="tpu_custom_call", output_to_operand_aliasing={{}: (1, {})} | custom-call | flops 102236160 | bytes 34078720 | tf_op jit(solution)/shard_map/collect_early/pallas_call | solution.py:569
  756.1 0.0 collective-permute-done.4.refs_2_
  756.1 0.7 collective-permute-done.5.refs_3_
  756.9 0.0 collective-permute-start.6
  756.9 0.5 collective-permute-start.7
  757.4 3.2 collect_late.1.refs_4_
  760.5 0.0 collective-permute-done.6.refs_2_
  760.5 0.0 collective-permute-done.7.refs_3_
  760.6 0.0 collective-permute-done.2.refs_0_
  760.6 0.0 collective-permute-done.3.refs_1_
  760.6 3.2 collect_last.1
Async XLA Ops:
  680.9 60.0 %collective-permute-start = (bf16[10400,128]{1,0:T(8,128)(2,1)}, bf16[10400,128]{1,0:T(8,128)(2,1)S(1)}, u32[]{:S(2)}, u32[]{:S(2)}) collective-permute-start(bf16[10400,128]{1,0:T(8,128)(2,1)} %get-tuple-element.36), channel_id=1, source_target_pairs={{0,2},{1,3},{2,0},{3,1},{4,6},{5,7},{6,4},{7,5}} | collective-permute-start | bytes 7987208 | tf_op jit(solution)/shard_map/ppermute | solution.py:615
  681.5 59.7 %collective-permute-start.1 = (bf16[10400,128]{1,0:T(8,128)(2,1)}, bf16[10400,128]{1,0:T(8,128)(2,1)S(1)}, u32[]{:S(2)}, u32[]{:S(2)}) collective-permute-start(bf16[10400,128]{1,0:T(8,128)(2,1)} %get-tuple-element.37), channel_id=1, source_target_pairs={{0,4},{1,5},{2,6},{3,7},{4,0},{5,1},{6,2},{7,3}} | collective-permute-start | bytes 7987208 | tf_op jit(solution)/shard_map/ppermute | solution.py:616
  682.9 20.3 %copy-start = (f32[8,6,128]{2,1,0:T(8,128)S(1)}, f32[8,6,128]{2,1,0:T(8,128)}, u32[]{:S(2)}) copy-start(f32[8,6,128]{2,1,0:T(8,128)} %get-tuple-element.42.vec_w) | copy-start | bytes 73732
  682.9 20.3 %copy-start.1 = (f32[3,6,128]{2,1,0:T(8,128)S(1)}, f32[3,6,128]{2,1,0:T(8,128)}, u32[]{:S(2)}) copy-start(f32[3,6,128]{2,1,0:T(8,128)} %get-tuple-element.41.vec_new) | copy-start | bytes 27652
  682.9 20.3 %copy-start.2 = (f32[8,128]{1,0:T(8,128)S(1)}, f32[8,128]{1,0:T(8,128)}, u32[]{:S(2)}) copy-start(f32[8,128]{1,0:T(8,128)} %get-tuple-element.39.coef) | copy-start | bytes 12292
  703.2 38.5 %copy-start.4 = (bf16[2080,128]{1,0:T(8,128)(2,1)S(1)}, bf16[2080,128]{1,0:T(8,128)(2,1)}, u32[]{:S(2)}) copy-start(bf16[2080,128]{1,0:T(8,128)(2,1)} %get-tuple-element.57) | copy-start | bytes 1597444
  703.2 39.9 %copy-start.3 = (bf16[2080,128]{1,0:T(8,128)(2,1)S(1)}, bf16[2080,128]{1,0:T(8,128)(2,1)}, u32[]{:S(2)}) copy-start(bf16[2080,128]{1,0:T(8,128)(2,1)} %get-tuple-element.58) | copy-start | bytes 1597444
  741.2 19.3 %collective-permute-start.2 = (bf16[10400,128]{1,0:T(8,128)(2,1)S(1)}, bf16[10400,128]{1,0:T(8,128)(2,1)S(1)}, u32[]{:S(2)}, u32[]{:S(2)}) collective-permute-start(bf16[10400,128]{1,0:T(8,128)(2,1)S(1)} %collective-permute-done.refs_0_), channel_id=1, source_target_pairs={{0,1},{1,0},{2,3},{3,2},{4,5},{5,4},{6,7},{7,6}} | collective-permute-start | bytes 7987208 | tf_op jit(solution)/shard_map/ppermute | solution.py:654
  741.2 19.3 %collective-permute-start.3 = (bf16[10400,128]{1,0:T(8,128)(2,1)S(1)}, bf16[10400,128]{1,0:T(8,128)(2,1)S(1)}, u32[]{:S(2)}, u32[]{:S(2)}) collective-permute-start(bf16[10400,128]{1,0:T(8,128)(2,1)S(1)} %collective-permute-done.1.refs_1_), channel_id=1, source_target_pairs={{0,1},{1,0},{2,3},{3,2},{4,5},{5,4},{6,7},{7,6}} | collective-permute-start | bytes 7987208 | tf_op jit(solution)/shard_map/ppermute | solution.py:655
  741.7 14.4 %collective-permute-start.4 = (bf16[2080,128]{1,0:T(8,128)(2,1)S(1)}, bf16[2080,128]{1,0:T(8,128)(2,1)S(1)}, u32[]{:S(2)}, u32[]{:S(2)}) collective-permute-start(bf16[2080,128]{1,0:T(8,128)(2,1)S(1)} %copy-done.4), channel_id=1, source_target_pairs={{0,2},{1,3},{2,0},{3,1},{4,6},{5,7},{6,4},{7,5}} | collective-permute-start | bytes 1597448 | tf_op jit(solution)/shard_map/ppermute | solution.py:617
  743.1 13.7 %collective-permute-start.5 = (bf16[2080,128]{1,0:T(8,128)(2,1)S(1)}, bf16[2080,128]{1,0:T(8,128)(2,1)S(1)}, u32[]{:S(2)}, u32[]{:S(2)}) collective-permute-start(bf16[2080,128]{1,0:T(8,128)(2,1)S(1)} %copy-done.3), channel_id=1, source_target_pairs={{0,4},{1,5},{2,6},{3,7},{4,0},{5,1},{6,2},{7,3}} | collective-permute-start | bytes 1597448 | tf_op jit(solution)/shard_map/ppermute | solution.py:618
  756.9 3.7 collective-permute-start.6
  756.9 3.7 collective-permute-start.7

commit v4 on v3

--- a/solution.py
+++ b/solution.py
@@ -6,6 +6,7 @@
 from jax.experimental import pallas as pl
 from jax.experimental.pallas import tpu as pltpu
 from jax.sharding import PartitionSpec as P
+
 
 STEP = 4
 LEARN_RATE = 1e-3
@@ -141,8 +142,14 @@
             device_id=(lax.rem(me + k, n_dev),), device_id_type=MESH)
 
     def send_sib(t):
-        for j in range(4):
-            sib_copy(j, t).start()
+        @pl.when(t < steps)
+        def _():
+            for j in range(3):
+                sib_copy(j, t).start()
+
+        @pl.when(t >= 1)
+        def _():
+            sib_copy(3, t - 1).start()
 
     def fetch(t, which):
         slot = lax.rem(t, 2)
@@ -170,22 +177,21 @@
         pl.semaphore_signal(barrier, inc=1, device_id=(lax.rem(me + k, n_dev),), device_id_type=MESH)
     fetch(jnp.int32(0), 0)
     pl.semaphore_wait(barrier, n_dev - 1)
-    send_sib(0)
-    send_sib(1)
+    send_sib(jnp.int32(0))
     acc[...] = jnp.zeros_like(acc)
     fetch(jnp.int32(0), 1)
+    send_sib(jnp.int32(1))
 
     @pl.loop(0, steps + 2)
     def _(t):
         slot = lax.rem(t, 2)
         before = 1 - slot
 
-        @pl.when(t + 2 < steps)
+        @pl.when(t + 2 <= steps)
         def _():
             send_sib(t + 2)
 
         fetch(t + 1, 0)
-        fetch(t + 1, 1)
 
         @pl.when(t < steps)
         def _():
@@ -194,6 +200,7 @@
                 @pl.when(t >= 2)
                 def _():
                     leaf_copy(t - 2, slot, part).wait_send()
+
                 store_pair(slot, part, leaf_st, part)
                 leaf_copy(t, slot, part).start()
             for part, piece, place in ((1, 'x_b', 2), (0, 'y_a', 3)):
@@ -202,8 +209,11 @@
                 @pl.when(t >= 2)
                 def _():
                     direct_copy(t - 2, slot, part).wait_send()
+
                 store_pair(slot, place, direct_st, part)
                 direct_copy(t, slot, part).start()
+
+        fetch(t + 1, 1)
 
         @pl.when(t == 0)
         def _():
@@ -221,12 +231,14 @@
                 @pl.when(t >= 3)
                 def _():
                     four_copy(t - 3, before, part).wait_send()
+
                 leaf_load(t - 1, part).wait()
 
                 @pl.loop(0, half // blk)
                 def _(i):
                     at = block_rows(i, part)
                     four_st[before, at, :] = leaf_in[at, :] + pair(slot, place, i)
+
                 four_copy(t - 1, before, part).start()
 
         @pl.when(t >= 2)
@@ -241,6 +253,7 @@
             @pl.when(t >= 4)
             def _():
                 out_copy(t - 4, slot).wait()
+
             fin_load(four_land, 0, t - 2).wait()
             fin_load(direct_land, 1, t - 2).wait()
 
@@ -250,6 +263,7 @@
                 whole = (fin_in[0, at, :] + fin_in[1, at, :]) + pair(slot, 6, i)
                 out_st[slot, at, :] = whole
                 acc[...] += jnp.sum((whole * whole).reshape(blk_rows // 8, 8, LANES), axis=0)
+
             out_copy(t - 2, slot).start()
 
     def square_copy(k):
@@ -373,6 +387,7 @@
                 @pl.when(u < early)
                 def _():
                     own_copy(1 - part, part, u).start()
+
                 own_copy(2, part, u).start()
                 keep_copy(part, u).start()
 
@@ -559,7 +574,7 @@
         give(k).wait()
 
 
-def copy_call(name, moves, srcs, out_rows, into=None, slots=12, most=4160):
+def copy_call(moves, srcs, out_rows, into=None, slots=12, most=4160):
     def blocks(n):
         return next(d for d in range(1, n // 16 + 1) if (n // 16) % d == 0 and n // d <= most)
 
@@ -576,7 +591,6 @@
         input_output_aliases={len(srcs): 0} if into is not None else {},
         compiler_params=pltpu.CompilerParams(vmem_limit_bytes=32 * 2**20),
         cost_estimate=pl.CostEstimate(flops=size * 6, bytes_accessed=2 * size, transcendentals=0),
-        name=name,
     )(*args)
 
 
@@ -585,8 +599,8 @@
 
 
 STEPS = 28
-W_STEPS = 14
-W_LATE = (10, 2)
+W_STEPS = 26
+W_LATE = (19, 6)
 LAG = 3
 
 
@@ -623,6 +637,14 @@
             flip = sib - me
             return [(0, dev * share_rows, dev * share_rows, share_rows) for dev in (me, sib, g_dev, g_dev + flip)]
 
+        def late_rows(x_dev, y_dev, first):
+            return [(first, 0, x_dev * share_rows + half_rows + early, late),
+                    (first + 1, 0, y_dev * share_rows + early, late)]
+
+        def last_rows(x_dev, y_dev, first):
+            return [(first, 0, x_dev * share_rows + half_rows + early + late, last),
+                    (first + 1, 0, y_dev * share_rows + early + late, last)]
+
         def early_moves(me):
             sib, x_dev, y_dev = neighbours(me)
             flip = sib - me
@@ -632,34 +654,30 @@
             for dev in (y_dev, y_dev + flip):
                 moves.append((0, dev * share_rows, dev * share_rows, early))
                 moves.append((0, dev * share_rows + half_rows, dev * share_rows + half_rows, half_rows))
-            return moves
-
-        def late_rows(x_dev, y_dev):
-            return [(0, 0, x_dev * share_rows + half_rows + early, late),
-                    (1, 0, y_dev * share_rows + early, late),
-                    (2, 0, x_dev * share_rows + half_rows + early + late, last),
-                    (3, 0, y_dev * share_rows + early + late, last)]
-
-        def own_late_moves(me):
-            _, x_dev, y_dev = neighbours(me)
-            return late_rows(x_dev, y_dev)
-
-        def sib_late_moves(me):
+            return moves + late_rows(x_dev, y_dev, 1)
+
+        def late_moves(me):
             sib, x_dev, y_dev = neighbours(me)
-            return late_rows(x_dev + sib - me, y_dev + sib - me)
+            flip = sib - me
+            return last_rows(x_dev, y_dev, 0) + late_rows(x_dev + flip, y_dev + flip, 2)
+
+        def last_moves(me):
+            sib, x_dev, y_dev = neighbours(me)
+            flip = sib - me
+            return last_rows(x_dev + flip, y_dev + flip, 0)
 
         *new, weights_vec = update_call(coef, total, *mats, vec_new, vec_w, block_rows_of(share_rows))
-        weights = copy_call('collect_whole', whole_moves, (gathered,), 8 * share_rows)
+        weights = copy_call(whole_moves, (gathered,), 8 * share_rows)
         late_x, late_y, weights, *new = lax.optimization_barrier((late_x, late_y, weights, *new))
         sib_late_x = lax.ppermute(late_x, 'fsdp', hop_core)
         sib_late_y = lax.ppermute(late_y, 'fsdp', hop_core)
-        weights = copy_call('collect_early', early_moves, (gathered,), 8 * share_rows, into=weights)
+        weights = copy_call(early_moves, (gathered, late_x, late_y), 8 * share_rows, into=weights)
         last_x, last_y, weights = lax.optimization_barrier((last_x, last_y, weights))
         sib_last_x = lax.ppermute(last_x, 'fsdp', hop_core)
         sib_last_y = lax.ppermute(last_y, 'fsdp', hop_core)
-        weights = copy_call('collect_late', own_late_moves, (late_x, late_y, last_x, last_y), 8 * share_rows, into=weights)
-        weights = copy_call('collect_last', sib_late_moves, (sib_late_x, sib_late_y, sib_last_x, sib_last_y),
-                            8 * share_rows, into=weights)
+        weights = copy_call(late_moves, (last_x, last_y, sib_late_x, sib_late_y), 8 * share_rows,
+                            into=weights)
+        weights = copy_call(last_moves, (sib_last_x, sib_last_y), 8 * share_rows, into=weights)
         return tuple(v.reshape(-1) for v in (*new, weights, weights_vec))
 
     row_spec = P('fsdp', None)

time: 766 us -> 763 us (level)
  Pallas kernels: 757 us -> 746 us
  waiting for transfers between devices: 1.16 us -> 8.82 us
    pallas_call x1, Pallas kernels: 680 us -> 670 us  [step_call(): pl.pallas_call(functools.partial(step_kernel, share, half, steps, w_steps...]
  transfers between devices with their start and end apart: 8 -> 8, of which waited for: 3 -> 4; matrix products, arithmetic and copies ran while one was open for 0% -> 0% of each run, Pallas kernels for 10% -> 10%
where the time goes in v4:
time: 763 us; the launch traced here: 761 us
  Pallas kernels  746 us (98%)
  waiting for transfers between devices  8.82 us (1%)
    pallas_call x1, Pallas kernels, step_call(): pl.pallas_call(functools.partial(step_kernel, share, half, steps, w_steps...  670 us
    pallas_call x4, Pallas kernels, copy_call(): pl.pallas_call(functools.partial(copy_kernel, moves, blocks), out_shape=j...  38.9 us
    pallas_call x1, Pallas kernels, update_call(): pl.pallas_call(update_kernel, grid=(n // block,), out_shape=(jax.ShapeDty...  37.6 us
  transfers between devices with their start and end apart: 8, of which 4 were waited for; matrix products, arithmetic and copies ran while one was open for 0% of the time, Pallas kernels for 10%

profile of v4, /device:TPU:0, one launch (start us, length us, event | category | flops | bytes accessed | tf_op | source)
XLA Modules:
  0.0 760.9 jit_solution(10936543459433306022)
XLA Ops:
  0.6 669.8 %reduce_update_gather.1 = (f32[29120,128]{1,0:T(8,128)}, bf16[232960,128]{1,0:T(8,128)(2,1)}, bf16[10640,128]{1,0:T(8,128)(2,1)}, bf16[10640,128]{1,0:T(8,128)(2...) custom-call(bf16[1,29818880]{1,0:T(2,128)(2,1)} %g.1, ...), custom_call_target="tpu_custom_call" | custom-call | tf_op jit(solution)/shard_map/reduce_update_gather/pallas_call | solution.py:462
  670.4 0.7 collective-permute-start
  671.1 1.3 collective-permute-start.1
  672.4 0.0 copy-start
  672.4 0.0 copy-start.1
  672.4 0.0 copy-start.2
  672.4 20.3 %shard_map.143.refs_3_ = bf16[232960,128]{1,0:T(8,128)(2,1)} custom-call(bf16[232960,128]{1,0:T(8,128)(2,1)} %get-tuple-element.38.refs_0_), custom_call_target="tpu_custom_call" | custom-call | flops 178913280 | bytes 59637760 | tf_op jit(solution)/shard_map/pallas_call | solution.py:584
  692.7 0.0 copy-done
  692.7 0.0 copy-done.1
  692.7 0.0 copy-done.2
  692.7 0.0 copy-start.4
  692.7 0.0 copy-start.3
  692.8 37.6 %update.1 = (f32[29120,128]{1,0:T(8,128)}, f32[29120,128]{1,0:T(8,128)}, f32[29120,128]{1,0:T(8,128)}, f32[6,128]{1,0:T(8,128)}, f32[6,128]{1,0:T(8,128)}, /*index=5*/f32[6,128]{1,0:T(8,128)}, bf16[48,128]{1,0:T(8,128)(2,1)}) custom-call(f32[8,128]{1,0:T(8,128)S(1)} %copy-done.2, f32[29120,128]{1,0:T(8,128)} %get-tuple-element.40.grad, ...), custom_call_target="tpu_custom_call" | custom-call | flops 745472000 | bytes 104366080 | tf_op jit(solution)/shard_map/update/pallas_call | solution.py:528
  730.4 1.6 collective-permute-done.refs_1_
  732.0 0.4 collective-permute-done.1.refs_2_
  732.3 0.0 collective-permute-start.6
  732.3 0.5 collective-permute-start.7
  732.8 0.0 copy-done.4
  732.8 1.4 collective-permute-start.2
  734.2 0.0 copy-done.3
  734.2 0.6 collective-permute-start.3
  734.9 13.3 %shard_map.144.refs_4_ = bf16[232960,128]{1,0:T(8,128)(2,1)} custom-call(bf16[232960,128]{1,0:T(8,128)(2,1)} %get-tuple-element.38.refs_0_, bf16[10640,128]{1,0:T(8,128)(2,1)S(1)} %collective-permute-done.refs_1_, bf16[10640,128]{1,0:T(8,128)(2,1)S(1)} %collective-permute-done.1.refs_2_, ...), custom_call_target="tpu_custom_call", output_to_operand_aliasing={{}: (3, {})} | custom-call | flops 125583360 | bytes 41861120 | tf_op jit(solution)/shard_map/pallas_call | solution.py:584
  748.1 5.7 collective-permute-done.2.refs_0_
  753.9 1.1 collective-permute-done.3.refs_1_
  755.0 0.0 collective-permute-start.4
  755.0 0.5 collective-permute-start.5
  755.5 0.0 collective-permute-done.6.refs_2_
  755.5 0.0 collective-permute-done.7.refs_3_
  755.5 3.7 shard_map.145.refs_2_
  759.2 0.0 collective-permute-done.4.refs_0_
  759.2 0.0 collective-permute-done.5.refs_1_
  759.2 1.7 shard_map.146
Async XLA Ops:
  670.4 61.6 %collective-permute-start = (bf16[10640,128]{1,0:T(8,128)(2,1)}, bf16[10640,128]{1,0:T(8,128)(2,1)S(1)}, u32[]{:S(2)}, u32[]{:S(2)}) collective-permute-start(bf16[10640,128]{1,0:T(8,128)(2,1)} %get-tuple-element.36), channel_id=1, source_target_pairs={{0,2},{1,3},{2,0},{3,1},{4,6},{5,7},{6,4},{7,5}} | collective-permute-start | bytes 8171528 | tf_op jit(solution)/shard_map/ppermute | solution.py:629
  671.1 61.3 %collective-permute-start.1 = (bf16[10640,128]{1,0:T(8,128)(2,1)}, bf16[10640,128]{1,0:T(8,128)(2,1)S(1)}, u32[]{:S(2)}, u32[]{:S(2)}) collective-permute-start(bf16[10640,128]{1,0:T(8,128)(2,1)} %get-tuple-element.37), channel_id=1, source_target_pairs={{0,4},{1,5},{2,6},{3,7},{4,0},{5,1},{6,2},{7,3}} | collective-permute-start | bytes 8171528 | tf_op jit(solution)/shard_map/ppermute | solution.py:630
  672.4 20.3 %copy-start = (f32[8,6,128]{2,1,0:T(8,128)S(1)}, f32[8,6,128]{2,1,0:T(8,128)}, u32[]{:S(2)}) copy-start(f32[8,6,128]{2,1,0:T(8,128)} %get-tuple-element.42.vec_w) | copy-start | bytes 73732
  672.4 20.3 %copy-start.1 = (f32[3,6,128]{2,1,0:T(8,128)S(1)}, f32[3,6,128]{2,1,0:T(8,128)}, u32[]{:S(2)}) copy-start(f32[3,6,128]{2,1,0:T(8,128)} %get-tuple-element.41.vec_new) | copy-start | bytes 27652
  672.4 20.3 %copy-start.2 = (f32[8,128]{1,0:T(8,128)S(1)}, f32[8,128]{1,0:T(8,128)}, u32[]{:S(2)}) copy-start(f32[8,128]{1,0:T(8,128)} %get-tuple-element.39.coef) | copy-start | bytes 12292
  692.7 40.1 %copy-start.4 = (bf16[3360,128]{1,0:T(8,128)(2,1)S(1)}, bf16[3360,128]{1,0:T(8,128)(2,1)}, u32[]{:S(2)}) copy-start(bf16[3360,128]{1,0:T(8,128)(2,1)} %get-tuple-element.55) | copy-start | bytes 2580484
  692.7 41.5 %copy-start.3 = (bf16[3360,128]{1,0:T(8,128)(2,1)S(1)}, bf16[3360,128]{1,0:T(8,128)(2,1)}, u32[]{:S(2)}) copy-start(bf16[3360,128]{1,0:T(8,128)(2,1)} %get-tuple-element.56) | copy-start | bytes 2580484
  732.3 23.2 %collective-permute-start.6 = (bf16[10640,128]{1,0:T(8,128)(2,1)S(1)}, bf16[10640,128]{1,0:T(8,128)(2,1)S(1)}, u32[]{:S(2)}, u32[]{:S(2)}) collective-permute-start(bf16[10640,128]{1,0:T(8,128)(2,1)S(1)} %collective-permute-done.refs_1_), channel_id=1, source_target_pairs={{0,1},{1,0},{2,3},{3,2},{4,5},{5,4},{6,7},{7,6}} | collective-permute-start | bytes 8171528 | tf_op jit(solution)/shard_map/ppermute | solution.py:672
  732.3 23.2 %collective-permute-start.7 = (bf16[10640,128]{1,0:T(8,128)(2,1)S(1)}, bf16[10640,128]{1,0:T(8,128)(2,1)S(1)}, u32[]{:S(2)}, u32[]{:S(2)}) collective-permute-start(bf16[10640,128]{1,0:T(8,128)(2,1)S(1)} %collective-permute-done.1.refs_2_), channel_id=1, source_target_pairs={{0,1},{1,0},{2,3},{3,2},{4,5},{5,4},{6,7},{7,6}} | collective-permute-start | bytes 8171528 | tf_op jit(solution)/shard_map/ppermute | solution.py:673
  732.8 21.0 %collective-permute-start.2 = (bf16[3360,128]{1,0:T(8,128)(2,1)S(1)}, bf16[3360,128]{1,0:T(8,128)(2,1)S(1)}, u32[]{:S(2)}, u32[]{:S(2)}) collective-permute-start(bf16[3360,128]{1,0:T(8,128)(2,1)S(1)} %copy-done.4), channel_id=1, source_target_pairs={{0,2},{1,3},{2,0},{3,1},{4,6},{5,7},{6,4},{7,5}} | collective-permute-start | bytes 2580488 | tf_op jit(solution)/shard_map/ppermute | solution.py:631
  734.2 20.7 %collective-permute-start.3 = (bf16[3360,128]{1,0:T(8,128)(2,1)S(1)}, bf16[3360,128]{1,0:T(8,128)(2,1)S(1)}, u32[]{:S(2)}, u32[]{:S(2)}) collective-permute-start(bf16[3360,128]{1,0:T(8,128)(2,1)S(1)} %copy-done.3), channel_id=1, source_target_pairs={{0,4},{1,5},{2,6},{3,7},{4,0},{5,1},{6,2},{7,3}} | collective-permute-start | bytes 2580488 | tf_op jit(solution)/shard_map/ppermute | solution.py:632
  755.0 4.2 collective-permute-start.4
  755.0 4.2 collective-permute-start.5

commit v5 on v4

--- a/solution.py
+++ b/solution.py
@@ -46,7 +46,7 @@
                   sib_send, sib_recv, leaf_send, leaf_recv, four_send, four_recv, direct_send, direct_recv,
                   own_sem, sibin_sem, leafin_sem, fin_sem, out_sem, sq_send, sq_recv, vec_send, vec_recv, local_sem,
                 state_in, own_w, state_sem, own_send, own_recv, own_sib_recv, keep_sem, late_sem,
-                fwd_send, fwd_recv, fsib_send, fsib_recv):
+                fwd_send, fwd_recv, fsib_send, fsib_recv, first_send, first_recv, vec_sum):
     me = lax.axis_index('fsdp')
     core = lax.rem(me, 2)
     x_pos = lax.rem(me // 2, 2)
@@ -66,6 +66,12 @@
         return pltpu.make_async_remote_copy(
             src_ref=g.at[:, pl.ds(src, 2 * half)], dst_ref=sib_land.at[:, pl.ds(dst, 2 * half)],
             send_sem=sib_send, recv_sem=sib_recv.at[j, t], device_id=(sib,), device_id_type=MESH)
+
+    def first_copy(part):
+        src = pl.multiple_of((g_dev + sib_delta) * share + part * half, TILE)
+        return pltpu.make_async_remote_copy(
+            src_ref=g.at[:, pl.ds(src, half)], dst_ref=raw_sib.at[0, :, pl.ds(part * half, half)],
+            send_sem=first_send.at[part], recv_sem=first_recv.at[part], device_id=(sib,), device_id_type=MESH)
 
     def raw_copy(piece, t, slot, which):
         place, width = PIECES[piece]
@@ -102,9 +108,9 @@
         return pltpu.make_async_copy(leaf_land.at[land_rows(t, part), :], leaf_in.at[pl.ds(part * rows, rows), :],
                                      leafin_sem.at[part])
 
-    def fin_load(land, which, t):
-        both = pl.ds(pl.multiple_of(t * 2 * rows, 8), 2 * rows)
-        return pltpu.make_async_copy(land.at[both, :], fin_in.at[which], fin_sem.at[which])
+    def fin_load(which, t, part):
+        return pltpu.make_async_copy((four_land, direct_land)[which].at[land_rows(t, part), :],
+                                     fin_in.at[which, pl.ds(part * rows, rows), :], fin_sem.at[which, part])
 
     def out_copy(t, slot):
         both = pl.ds(pl.multiple_of(t * 2 * rows, 8), 2 * rows)
@@ -131,10 +137,16 @@
         for which in range(2):
             raw_copy(piece, t, slot, which).wait()
 
+    own_rows = pv.shape[0]
+
+    def row_part(dev):
+        return gv.at[:, pl.ds(pl.multiple_of(dev * own_rows * LANES, LANES), own_rows * LANES)]
+
     def row_copy(k):
-        return pltpu.make_async_remote_copy(
-            src_ref=gv, dst_ref=vec_land.at[me], send_sem=vec_send.at[k - 1, 0], recv_sem=vec_recv.at[k - 1, 0],
-            device_id=(lax.rem(me + k, n_dev),), device_id_type=MESH)
+        target = lax.rem(me + k, n_dev)
+        return pltpu.make_async_remote_copy(
+            src_ref=row_part(target), dst_ref=vec_land.at[me], send_sem=vec_send.at[k - 1, 0],
+            recv_sem=vec_recv.at[k - 1, 0], device_id=(target,), device_id_type=MESH)
 
     def new_copy(k):
         return pltpu.make_async_remote_copy(
@@ -142,9 +154,13 @@
             device_id=(lax.rem(me + k, n_dev),), device_id_type=MESH)
 
     def send_sib(t):
+        @pl.when(jnp.logical_and(t >= 1, t < steps))
+        def _():
+            sib_copy(0, t).start()
+
         @pl.when(t < steps)
         def _():
-            for j in range(3):
+            for j in range(1, 3):
                 sib_copy(j, t).start()
 
         @pl.when(t >= 1)
@@ -154,9 +170,15 @@
     def fetch(t, which):
         slot = lax.rem(t, 2)
 
+        @pl.when(jnp.logical_and(t >= which, t < steps))
+        def _():
+            if which == 1:
+                sib_copy(0, t).wait_recv()
+            raw_copy('diag', t, slot, which).start()
+
         @pl.when(t < steps)
         def _():
-            for j, piece in enumerate(('diag', 'x_b', 'y_a')):
+            for j, piece in ((1, 'x_b'), (2, 'y_a')):
                 if which == 1:
                     sib_copy(j, t).wait_recv()
                 raw_copy(piece, t, slot, which).start()
@@ -177,9 +199,10 @@
         pl.semaphore_signal(barrier, inc=1, device_id=(lax.rem(me + k, n_dev),), device_id_type=MESH)
     fetch(jnp.int32(0), 0)
     pl.semaphore_wait(barrier, n_dev - 1)
+    for part in range(2):
+        first_copy(part).start()
     send_sib(jnp.int32(0))
     acc[...] = jnp.zeros_like(acc)
-    fetch(jnp.int32(0), 1)
     send_sib(jnp.int32(1))
 
     @pl.loop(0, steps + 2)
@@ -195,14 +218,28 @@
 
         @pl.when(t < steps)
         def _():
-            wait_raw('diag', t, slot)
+            raw_copy('diag', t, slot, 0).wait()
+
+            @pl.when(t >= 1)
+            def _():
+                raw_copy('diag', t, slot, 1).wait()
+
             for part in range(2):
+                @pl.when(t == 0)
+                def _():
+                    first_copy(part).wait_recv()
+
                 @pl.when(t >= 2)
                 def _():
                     leaf_copy(t - 2, slot, part).wait_send()
 
                 store_pair(slot, part, leaf_st, part)
                 leaf_copy(t, slot, part).start()
+
+            @pl.when(t == 0)
+            def _():
+                fetch(t, 1)
+
             for part, piece, place in ((1, 'x_b', 2), (0, 'y_a', 3)):
                 wait_raw(piece, t, slot)
 
@@ -219,6 +256,19 @@
         def _():
             for k in range(1, n_dev):
                 row_copy(k).start()
+            pltpu.make_async_copy(row_part(me), vec_land.at[me], local_sem).start()
+
+        @pl.when(t == 3)
+        def _():
+            for k in range(1, n_dev):
+                row_copy(k).wait()
+            pltpu.make_async_copy(row_part(me), vec_land.at[me], local_sem).wait()
+            part_sum = vec_land[0].astype(jnp.float32)
+            for d in range(1, n_dev):
+                part_sum += vec_land[d].astype(jnp.float32)
+            part_sum = part_sum.reshape(own_rows, LANES)
+            vec_sum[...] = part_sum
+            acc[0:own_rows, :] += part_sum * part_sum
 
         @pl.when(jnp.logical_and(t >= 1, t <= steps))
         def _():
@@ -244,26 +294,26 @@
         @pl.when(t >= 2)
         def _():
             for part in range(2):
-                four_copy(t - 2, slot, part).wait_recv()
                 direct_copy(t - 2, slot, part).wait_recv()
-            fin_load(four_land, 0, t - 2).start()
-            fin_load(direct_land, 1, t - 2).start()
+                fin_load(1, t - 2, part).start()
             wait_raw('mine', t - 2, slot)
 
             @pl.when(t >= 4)
             def _():
                 out_copy(t - 4, slot).wait()
 
-            fin_load(four_land, 0, t - 2).wait()
-            fin_load(direct_land, 1, t - 2).wait()
-
-            @pl.loop(0, 2 * half // blk)
-            def _(i):
-                at = block_rows(i)
-                whole = (fin_in[0, at, :] + fin_in[1, at, :]) + pair(slot, 6, i)
-                out_st[slot, at, :] = whole
-                acc[...] += jnp.sum((whole * whole).reshape(blk_rows // 8, 8, LANES), axis=0)
-
+            for part in range(2):
+                four_copy(t - 2, slot, part).wait_recv()
+                fin_load(0, t - 2, part).start()
+                fin_load(1, t - 2, part).wait()
+                fin_load(0, t - 2, part).wait()
+
+                @pl.loop(0, half // blk)
+                def _(i):
+                    at = block_rows(i, part)
+                    whole = (fin_in[0, at, :] + fin_in[1, at, :]) + pair(slot, 6 + part, i)
+                    out_st[slot, at, :] = whole
+                    acc[...] += jnp.sum((whole * whole).reshape(blk_rows // 8, 8, LANES), axis=0)
             out_copy(t - 2, slot).start()
 
     def square_copy(k):
@@ -277,9 +327,6 @@
     sq_land[me] = acc[...]
     for t in (steps - 2, steps - 1):
         out_copy(t, t % 2).wait()
-    own_row = pltpu.make_async_copy(gv, vec_land.at[me], local_sem)
-    own_row.start()
-
     share_rows = share // LANES
     half_rows = share_rows // 2
     w_rows = half_rows // w_steps
@@ -330,21 +377,7 @@
     for copy in state_copies(0, 0):
         copy.start()
 
-    own_row.wait()
-    for k in range(1, n_dev):
-        row_copy(k).wait()
-    vec_total = vec_land[0].astype(jnp.float32)
-    for d in range(1, n_dev):
-        vec_total += vec_land[d].astype(jnp.float32)
-    vec_rows = gv.shape[1] // LANES
-    vec_total = vec_total.reshape(vec_rows, LANES)
-    square = jnp.sum((vec_total * vec_total).reshape(vec_rows // 8, 8, LANES), axis=0)
-    own_rows = pv.shape[0]
-    mine = pl.ds(pl.multiple_of(me * own_rows * LANES, LANES), own_rows * LANES)
-    vec_sum = vec_land[0, :, mine].astype(jnp.float32)
-    for d in range(1, n_dev):
-        vec_sum += vec_land[d, :, mine].astype(jnp.float32)
-    vec_sum = vec_sum.reshape(own_rows, LANES)
+    square = jnp.zeros_like(acc)
     for k in range(1, n_dev):
         square_copy(k).wait()
     for d in range(n_dev):
@@ -414,7 +447,7 @@
 
         @pl.when(u == 1)
         def _():
-            new = adam_update(vec_sum, coef_out[0:1, :], pv[...], mv[...], sv[...], 0.0)
+            new = adam_update(vec_sum[...], coef_out[0:1, :], pv[...], mv[...], sv[...], 0.0)
             for i in range(3):
                 vec_new[i] = new[i]
             vec_w[me] = new[0]
@@ -437,8 +470,10 @@
             direct_copy(t, slot, part).wait_send()
             four_copy(t, slot, part).wait_send()
     pltpu.make_async_remote_copy(
-        src_ref=g.at[:, pl.ds(0, 4 * share)], dst_ref=sib_land, send_sem=sib_send, recv_sem=sib_recv.at[0, 0],
-        device_id=(sib,), device_id_type=MESH).wait_send()
+        src_ref=g.at[:, pl.ds(0, 4 * share - 2 * half)], dst_ref=sib_land.at[:, pl.ds(0, 4 * share - 2 * half)],
+        send_sem=sib_send, recv_sem=sib_recv.at[0, 0], device_id=(sib,), device_id_type=MESH).wait_send()
+    for part in range(2):
+        first_copy(part).wait_send()
     for part in range(2):
         late_copy(0, part).wait()
         late_copy(1, part).wait()
@@ -487,15 +522,16 @@
             pltpu.VMEM((2, 2 * rows, LANES), f32),
             pltpu.VMEM((8, LANES), f32),
             pltpu.VMEM((8, 8, LANES), f32),
-            pltpu.VMEM((8, 1, gv.shape[1]), bf16),
+            pltpu.VMEM((8, 1, own_rows * LANES), bf16),
             dma(()), dma((4, steps)),
             dma((2, 2)), dma((2, steps)), dma((2, 2)), dma((2, steps)), dma((2, 2)), dma((2, steps)),
-            dma((2, 6)), dma((2, 6)), dma((2,)), dma((2,)), dma((2,)),
+            dma((2, 6)), dma((2, 6)), dma((2,)), dma((2, 2)), dma((2,)),
             dma((7,)), dma((7,)), dma((7, 2)), dma((7, 2)), dma(()),
             pltpu.VMEM((2, 4, 2, w_rows, LANES), f32),
             pltpu.VMEM((share_rows, LANES), bf16),
             dma((2, 4, 2)), dma((3,)), dma((2, 2, w_steps)), dma(()), dma(()), dma((2, 2)),
-            dma((2,)), dma((2, w_steps)), dma(()), dma(()),
+            dma((2,)), dma((2, w_steps)), dma(()), dma(()), dma((2,)), dma((2,)),
+            pltpu.VMEM((own_rows, LANES), f32),
         ],
         compiler_params=pltpu.CompilerParams(collective_id=0, has_side_effects=True, vmem_limit_bytes=60 * 2**20),
         name='reduce_update_gather',
@@ -635,7 +671,8 @@
             sib, x_dev, y_dev = neighbours(me)
             g_dev = x_dev + y_dev - me
             flip = sib - me
-            return [(0, dev * share_rows, dev * share_rows, share_rows) for dev in (me, sib, g_dev, g_dev + flip)]
+            return [(0, dev * share_rows, dev * share_rows, share_rows) for dev in (me, sib, g_dev, g_dev + flip)] + [
+                (0, x_dev * share_rows, x_dev * share_rows, half_rows)]
 
         def late_rows(x_dev, y_dev, first):
             return [(first, 0, x_dev * share_rows + half_rows + early, late),
@@ -648,18 +685,23 @@
         def early_moves(me):
             sib, x_dev, y_dev = neighbours(me)
             flip = sib - me
-            moves = []
+            moves = [(0, (x_dev + flip) * share_rows, (x_dev + flip) * share_rows, half_rows)]
             for dev in (x_dev, x_dev + flip):
-                moves.append((0, dev * share_rows, dev * share_rows, half_rows + early))
+                start = dev * share_rows + half_rows
+                moves.append((0, start, start, early))
             for dev in (y_dev, y_dev + flip):
-                moves.append((0, dev * share_rows, dev * share_rows, early))
-                moves.append((0, dev * share_rows + half_rows, dev * share_rows + half_rows, half_rows))
+                start = dev * share_rows
+                moves.append((0, start, start, early))
+                moves.append((0, start + half_rows, start + half_rows, half_rows))
             return moves + late_rows(x_dev, y_dev, 1)
 
+        def mid_moves(me):
+            sib, x_dev, y_dev = neighbours(me)
+            return late_rows(x_dev + sib - me, y_dev + sib - me, 0)
+
         def late_moves(me):
-            sib, x_dev, y_dev = neighbours(me)
-            flip = sib - me
-            return last_rows(x_dev, y_dev, 0) + late_rows(x_dev + flip, y_dev + flip, 2)
+            _, x_dev, y_dev = neighbours(me)
+            return last_rows(x_dev, y_dev, 0)
 
         def last_moves(me):
             sib, x_dev, y_dev = neighbours(me)
@@ -672,11 +714,11 @@
         sib_late_x = lax.ppermute(late_x, 'fsdp', hop_core)
         sib_late_y = lax.ppermute(late_y, 'fsdp', hop_core)
         weights = copy_call(early_moves, (gathered, late_x, late_y), 8 * share_rows, into=weights)
+        weights = copy_call(mid_moves, (sib_late_x, sib_late_y), 8 * share_rows, into=weights)
         last_x, last_y, weights = lax.optimization_barrier((last_x, last_y, weights))
         sib_last_x = lax.ppermute(last_x, 'fsdp', hop_core)
         sib_last_y = lax.ppermute(last_y, 'fsdp', hop_core)
-        weights = copy_call(late_moves, (last_x, last_y, sib_late_x, sib_late_y), 8 * share_rows,
-                            into=weights)
+        weights = copy_call(late_moves, (last_x, last_y), 8 * share_rows, into=weights)
         weights = copy_call(last_moves, (sib_last_x, sib_last_y), 8 * share_rows, into=weights)
         return tuple(v.reshape(-1) for v in (*new, weights, weights_vec))
 

time: 763 us -> 760 us (level)
    pallas_call x4 -> x5, Pallas kernels: 38.9 us -> 39.4 us  [copy_call(): pl.pallas_call(functools.partial(copy_kernel, moves, blocks), out_shape=j...]
where the time goes in v5:
time: 760 us; the launch traced here: 757 us
  Pallas kernels  744 us (98%)
  waiting for transfers between devices  7.64 us (1%)
    pallas_call x1, Pallas kernels, step_call(): pl.pallas_call(functools.partial(step_kernel, share, half, steps, w_steps...  667 us
    pallas_call x5, Pallas kernels, copy_call(): pl.pallas_call(functools.partial(copy_kernel, moves, blocks), out_shape=j...  39.4 us
    pallas_call x1, Pallas kernels, update_call(): pl.pallas_call(update_kernel, grid=(n // block,), out_shape=(jax.ShapeDty...  37.6 us
  transfers between devices with their start and end apart: 8, of which 4 were waited for; matrix products, arithmetic and copies ran while one was open for 0% of the time, Pallas kernels for 10%

profile of v5, /device:TPU:0, one launch (start us, length us, event | category | flops | bytes accessed | tf_op | source)
XLA Modules:
  0.0 757.4 jit_solution(15769686836323753511)
XLA Ops:
  0.6 666.9 %reduce_update_gather.1 = (f32[29120,128]{1,0:T(8,128)}, bf16[232960,128]{1,0:T(8,128)(2,1)}, bf16[10640,128]{1,0:T(8,128)(2,1)}, bf16[10640,128]{1,0:T(8,128)(2...) custom-call(bf16[1,29818880]{1,0:T(2,128)(2,1)} %g.1, ...), custom_call_target="tpu_custom_call" | custom-call | tf_op jit(solution)/shard_map/reduce_update_gather/pallas_call | solution.py:497
  667.5 0.7 collective-permute-start
  668.2 1.2 collective-permute-start.1
  669.4 0.0 copy-start
  669.4 0.0 copy-start.1
  669.4 0.0 copy-start.2
  669.4 22.6 %shard_map.143.refs_3_ = bf16[232960,128]{1,0:T(8,128)(2,1)} custom-call(bf16[232960,128]{1,0:T(8,128)(2,1)} %get-tuple-element.38.refs_0_), custom_call_target="tpu_custom_call" | custom-call | flops 201277440 | bytes 67092480 | tf_op jit(solution)/shard_map/pallas_call | solution.py:620
  692.0 0.0 copy-done
  692.0 0.0 copy-done.1
  692.0 0.0 copy-done.2
  692.0 0.0 copy-start.4
  692.0 0.0 copy-start.3
  692.0 37.6 %update.1 = (f32[29120,128]{1,0:T(8,128)}, f32[29120,128]{1,0:T(8,128)}, f32[29120,128]{1,0:T(8,128)}, f32[6,128]{1,0:T(8,128)}, f32[6,128]{1,0:T(8,128)}, /*index=5*/f32[6,128]{1,0:T(8,128)}, bf16[48,128]{1,0:T(8,128)(2,1)}) custom-call(f32[8,128]{1,0:T(8,128)S(1)} %copy-done.2, f32[29120,128]{1,0:T(8,128)} %get-tuple-element.40.grad, ...), custom_call_target="tpu_custom_call" | custom-call | flops 745472000 | bytes 104366080 | tf_op jit(solution)/shard_map/update/pallas_call | solution.py:564
  729.6 0.0 collective-permute-done.refs_1_
  729.6 0.0 collective-permute-done.1.refs_2_
  729.6 0.0 collective-permute-start.4
  729.7 0.5 collective-permute-start.5
  730.2 0.0 copy-done.4
  730.2 1.2 collective-permute-start.2
  731.3 0.0 copy-done.3
  731.3 1.1 collective-permute-start.3
  732.4 10.4 %shard_map.144.refs_2_ = bf16[232960,128]{1,0:T(8,128)(2,1)} custom-call(bf16[232960,128]{1,0:T(8,128)(2,1)} %get-tuple-element.38.refs_0_, bf16[10640,128]{1,0:T(8,128)(2,1)S(1)} %collective-permute-done.refs_1_, bf16[10640,128]{1,0:T(8,128)(2,1)S(1)} %collective-permute-done.1.refs_2_, ...), custom_call_target="tpu_custom_call", output_to_operand_aliasing={{}: (3, {})} | custom-call | flops 103219200 | bytes 34406400 | tf_op jit(solution)/shard_map/pallas_call | solution.py:620
  742.8 0.0 collective-permute-done.4.refs_0_
  742.8 0.0 collective-permute-done.5.refs_1_
  742.8 3.0 shard_map.145.refs_2_
  745.9 5.4 collective-permute-done.2.refs_0_
  751.2 0.8 collective-permute-done.3.refs_1_
  752.1 0.0 collective-permute-start.6
  752.1 0.5 collective-permute-start.7
  752.6 1.7 shard_map.146.refs_2_
  754.3 0.2 collective-permute-done.6.refs_0_
  754.5 1.2 collective-permute-done.7.refs_1_
  755.7 1.7 shard_map.147
Async XLA Ops:
  667.5 62.1 %collective-permute-start = (bf16[10640,128]{1,0:T(8,128)(2,1)}, bf16[10640,128]{1,0:T(8,128)(2,1)S(1)}, u32[]{:S(2)}, u32[]{:S(2)}) collective-permute-start(bf16[10640,128]{1,0:T(8,128)(2,1)} %get-tuple-element.36), channel_id=1, source_target_pairs={{0,2},{1,3},{2,0},{3,1},{4,6},{5,7},{6,4},{7,5}} | collective-permute-start | bytes 8171528 | tf_op jit(solution)/shard_map/ppermute | solution.py:665
  668.2 61.5 %collective-permute-start.1 = (bf16[10640,128]{1,0:T(8,128)(2,1)}, bf16[10640,128]{1,0:T(8,128)(2,1)S(1)}, u32[]{:S(2)}, u32[]{:S(2)}) collective-permute-start(bf16[10640,128]{1,0:T(8,128)(2,1)} %get-tuple-element.37), channel_id=1, source_target_pairs={{0,4},{1,5},{2,6},{3,7},{4,0},{5,1},{6,2},{7,3}} | collective-permute-start | bytes 8171528 | tf_op jit(solution)/shard_map/ppermute | solution.py:666
  669.4 22.6 %copy-start = (f32[8,6,128]{2,1,0:T(8,128)S(1)}, f32[8,6,128]{2,1,0:T(8,128)}, u32[]{:S(2)}) copy-start(f32[8,6,128]{2,1,0:T(8,128)} %get-tuple-element.42.vec_w) | copy-start | bytes 73732
  669.4 22.6 %copy-start.1 = (f32[3,6,128]{2,1,0:T(8,128)S(1)}, f32[3,6,128]{2,1,0:T(8,128)}, u32[]{:S(2)}) copy-start(f32[3,6,128]{2,1,0:T(8,128)} %get-tuple-element.41.vec_new) | copy-start | bytes 27652
  669.4 22.6 %copy-start.2 = (f32[8,128]{1,0:T(8,128)S(1)}, f32[8,128]{1,0:T(8,128)}, u32[]{:S(2)}) copy-start(f32[8,128]{1,0:T(8,128)} %get-tuple-element.39.coef) | copy-start | bytes 12292
  692.0 38.2 %copy-start.4 = (bf16[3360,128]{1,0:T(8,128)(2,1)S(1)}, bf16[3360,128]{1,0:T(8,128)(2,1)}, u32[]{:S(2)}) copy-start(bf16[3360,128]{1,0:T(8,128)(2,1)} %get-tuple-element.55) | copy-start | bytes 2580484
  692.0 39.3 %copy-start.3 = (bf16[3360,128]{1,0:T(8,128)(2,1)S(1)}, bf16[3360,128]{1,0:T(8,128)(2,1)}, u32[]{:S(2)}) copy-start(bf16[3360,128]{1,0:T(8,128)(2,1)} %get-tuple-element.56) | copy-start | bytes 2580484
  729.6 13.2 %collective-permute-start.4 = (bf16[10640,128]{1,0:T(8,128)(2,1)S(1)}, bf16[10640,128]{1,0:T(8,128)(2,1)S(1)}, u32[]{:S(2)}, u32[]{:S(2)}) collective-permute-start(bf16[10640,128]{1,0:T(8,128)(2,1)S(1)} %collective-permute-done.refs_1_), channel_id=1, source_target_pairs={{0,1},{1,0},{2,3},{3,2},{4,5},{5,4},{6,7},{7,6}} | collective-permute-start | bytes 8171528 | tf_op jit(solution)/shard_map/ppermute | solution.py:714
  729.7 13.2 %collective-permute-start.5 = (bf16[10640,128]{1,0:T(8,128)(2,1)S(1)}, bf16[10640,128]{1,0:T(8,128)(2,1)S(1)}, u32[]{:S(2)}, u32[]{:S(2)}) collective-permute-start(bf16[10640,128]{1,0:T(8,128)(2,1)S(1)} %collective-permute-done.1.refs_2_), channel_id=1, source_target_pairs={{0,1},{1,0},{2,3},{3,2},{4,5},{5,4},{6,7},{7,6}} | collective-permute-start | bytes 8171528 | tf_op jit(solution)/shard_map/ppermute | solution.py:715
  730.2 21.1 %collective-permute-start.2 = (bf16[3360,128]{1,0:T(8,128)(2,1)S(1)}, bf16[3360,128]{1,0:T(8,128)(2,1)S(1)}, u32[]{:S(2)}, u32[]{:S(2)}) collective-permute-start(bf16[3360,128]{1,0:T(8,128)(2,1)S(1)} %copy-done.4), channel_id=1, source_target_pairs={{0,2},{1,3},{2,0},{3,1},{4,6},{5,7},{6,4},{7,5}} | collective-permute-start | bytes 2580488 | tf_op jit(solution)/shard_map/ppermute | solution.py:667
  731.3 20.7 %collective-permute-start.3 = (bf16[3360,128]{1,0:T(8,128)(2,1)S(1)}, bf16[3360,128]{1,0:T(8,128)(2,1)S(1)}, u32[]{:S(2)}, u32[]{:S(2)}) collective-permute-start(bf16[3360,128]{1,0:T(8,128)(2,1)S(1)} %copy-done.3), channel_id=1, source_target_pairs={{0,4},{1,5},{2,6},{3,7},{4,0},{5,1},{6,2},{7,3}} | collective-permute-start | bytes 2580488 | tf_op jit(solution)/shard_map/ppermute | solution.py:668
  752.1 2.4 collective-permute-start.6
  752.1 3.6 collective-permute-start.7

commit v6 on v5

--- a/solution.py
+++ b/solution.py
@@ -581,6 +581,8 @@
     me = lax.axis_index('fsdp')
     todo = []
     for which, src_row, dst_row, n in moves(me):
+        if n == 0:
+            continue
         size = n // blocks(n)
         for i in range(blocks(n)):
             todo.append((srcs[which], src_row + i * size, dst_row + i * size, size))
@@ -610,7 +612,7 @@
         give(k).wait()
 
 
-def copy_call(moves, srcs, out_rows, into=None, slots=12, most=4160):
+def copy_call(moves, srcs, out_rows, into=None, slots=6, most=14560):
     def blocks(n):
         return next(d for d in range(1, n // 16 + 1) if (n // 16) % d == 0 and n // d <= most)
 
@@ -630,6 +632,31 @@
     )(*args)
 
 
+def place_kernel(moves, *refs):
+    out, sems = refs[-2], refs[-1]
+    copies = [pltpu.make_async_copy(refs[which], out.at[pl.ds(pl.multiple_of(dst_row, 16), n), :], sems.at[i])
+              for i, (which, _, dst_row, n) in enumerate(moves(lax.axis_index('fsdp')))]
+    for copy in copies:
+        copy.start()
+    for copy in copies:
+        copy.wait()
+
+
+def place_call(moves, srcs, into):
+    hbm, vmem = pl.BlockSpec(memory_space=pltpu.HBM), pl.BlockSpec(memory_space=pltpu.VMEM)
+    size = sum(move[3] for move in moves(0)) * LANES * 2
+    return pl.pallas_call(
+        functools.partial(place_kernel, moves),
+        out_shape=jax.ShapeDtypeStruct(into.shape, into.dtype),
+        in_specs=[vmem] * len(srcs) + [hbm],
+        out_specs=hbm,
+        scratch_shapes=[pltpu.SemaphoreType.DMA((len(srcs),))],
+        input_output_aliases={len(srcs): 0},
+        compiler_params=pltpu.CompilerParams(vmem_limit_bytes=16 * 2**20),
+        cost_estimate=pl.CostEstimate(flops=size * 6, bytes_accessed=2 * size, transcendentals=0),
+    )(*srcs, into)
+
+
 def block_rows_of(n):
     return 16 * max(d for d in range(1, 190) if (n // 16) % d == 0)
 
@@ -714,12 +741,12 @@
         sib_late_x = lax.ppermute(late_x, 'fsdp', hop_core)
         sib_late_y = lax.ppermute(late_y, 'fsdp', hop_core)
         weights = copy_call(early_moves, (gathered, late_x, late_y), 8 * share_rows, into=weights)
-        weights = copy_call(mid_moves, (sib_late_x, sib_late_y), 8 * share_rows, into=weights)
+        weights = place_call(mid_moves, (sib_late_x, sib_late_y), weights)
         last_x, last_y, weights = lax.optimization_barrier((last_x, last_y, weights))
         sib_last_x = lax.ppermute(last_x, 'fsdp', hop_core)
         sib_last_y = lax.ppermute(last_y, 'fsdp', hop_core)
-        weights = copy_call(late_moves, (last_x, last_y), 8 * share_rows, into=weights)
-        weights = copy_call(last_moves, (sib_last_x, sib_last_y), 8 * share_rows, into=weights)
+        weights = place_call(late_moves, (last_x, last_y), weights)
+        weights = place_call(last_moves, (sib_last_x, sib_last_y), weights)
         return tuple(v.reshape(-1) for v in (*new, weights, weights_vec))
 
     row_spec = P('fsdp', None)

time: 760 us -> 760 us (level)
    pallas_call x5 -> x2, Pallas kernels: 39.4 us -> 34.3 us  [copy_call(): pl.pallas_call(functools.partial(copy_kernel, moves, blocks), out_shape=j...]
where the time goes in v6:
time: 760 us; the launch traced here: 757 us
  Pallas kernels  744 us (98%)
  waiting for transfers between devices  7.81 us (1%)
    pallas_call x1, Pallas kernels, step_call(): pl.pallas_call(functools.partial(step_kernel, share, half, steps, w_steps...  667 us
    pallas_call x1, Pallas kernels, update_call(): pl.pallas_call(update_kernel, grid=(n // block,), out_shape=(jax.ShapeDty...  37.6 us
    pallas_call x2, Pallas kernels, copy_call(): pl.pallas_call(functools.partial(copy_kernel, moves, blocks), out_shape=j...  34.3 us
  transfers between devices with their start and end apart: 8, of which 4 were waited for; matrix products, arithmetic and copies ran while one was open for 0% of the time, Pallas kernels for 10%

profile of v6, /device:TPU:0, one launch (start us, length us, event | category | flops | bytes accessed | tf_op | source)
XLA Modules:
  0.0 757.4 jit_solution(12573119784524640229)
XLA Ops:
  0.6 666.9 %reduce_update_gather.1 = (f32[29120,128]{1,0:T(8,128)}, bf16[232960,128]{1,0:T(8,128)(2,1)}, bf16[10640,128]{1,0:T(8,128)(2,1)}, bf16[10640,128]{1,0:T(8,128)(2...) custom-call(bf16[1,29818880]{1,0:T(2,128)(2,1)} %g.1, ...), custom_call_target="tpu_custom_call" | custom-call | tf_op jit(solution)/shard_map/reduce_update_gather/pallas_call | solution.py:497
  667.5 0.7 collective-permute-start
  668.2 1.2 collective-permute-start.1
  669.4 0.0 copy-start
  669.4 0.0 copy-start.1
  669.4 0.0 copy-start.2
  669.4 23.3 %shard_map.143.refs_3_ = bf16[232960,128]{1,0:T(8,128)(2,1)} custom-call(bf16[232960,128]{1,0:T(8,128)(2,1)} %get-tuple-element.38.refs_0_), custom_call_target="tpu_custom_call" | custom-call | flops 201277440 | bytes 67092480 | tf_op jit(solution)/shard_map/pallas_call | solution.py:622
  692.7 0.0 copy-done
  692.7 0.0 copy-done.1
  692.7 0.0 copy-done.2
  692.7 0.0 copy-start.4
  692.7 0.0 copy-start.3
  692.7 37.6 %update.1 = (f32[29120,128]{1,0:T(8,128)}, f32[29120,128]{1,0:T(8,128)}, f32[29120,128]{1,0:T(8,128)}, f32[6,128]{1,0:T(8,128)}, f32[6,128]{1,0:T(8,128)}, /*index=5*/f32[6,128]{1,0:T(8,128)}, bf16[48,128]{1,0:T(8,128)(2,1)}) custom-call(f32[8,128]{1,0:T(8,128)S(1)} %copy-done.2, f32[29120,128]{1,0:T(8,128)} %get-tuple-element.40.grad, ...), custom_call_target="tpu_custom_call" | custom-call | flops 745472000 | bytes 104366080 | tf_op jit(solution)/shard_map/update/pallas_call | solution.py:564
  730.4 0.0 collective-permute-done.refs_1_
  730.4 0.0 collective-permute-done.1.refs_2_
  730.4 0.0 collective-permute-start.4
  730.4 0.5 collective-permute-start.5
  730.9 0.0 copy-done.4
  730.9 0.8 collective-permute-start.2
  731.8 0.0 copy-done.3
  731.8 1.4 collective-permute-start.3
  733.1 11.0 %shard_map.144.refs_2_ = bf16[232960,128]{1,0:T(8,128)(2,1)} custom-call(bf16[232960,128]{1,0:T(8,128)(2,1)} %get-tuple-element.38.refs_0_, bf16[10640,128]{1,0:T(8,128)(2,1)S(1)} %collective-permute-done.refs_1_, bf16[10640,128]{1,0:T(8,128)(2,1)S(1)} %collective-permute-done.1.refs_2_, ...), custom_call_target="tpu_custom_call", output_to_operand_aliasing={{}: (3, {})} | custom-call | flops 103219200 | bytes 34406400 | tf_op jit(solution)/shard_map/pallas_call | solution.py:622
  744.1 0.0 collective-permute-done.4.refs_0_
  744.2 0.0 collective-permute-done.5.refs_1_
  744.2 2.5 shard_map.145.refs_2_
  746.6 5.3 collective-permute-done.2.refs_0_
  752.0 0.6 collective-permute-done.3.refs_1_
  752.5 0.0 collective-permute-start.6
  752.5 0.5 collective-permute-start.7
  753.0 1.2 shard_map.146.refs_2_
  754.3 0.7 collective-permute-done.6.refs_0_
  754.9 1.2 collective-permute-done.7.refs_1_
  756.2 1.2 shard_map.147
Async XLA Ops:
  667.5 62.9 %collective-permute-start = (bf16[10640,128]{1,0:T(8,128)(2,1)}, bf16[10640,128]{1,0:T(8,128)(2,1)S(1)}, u32[]{:S(2)}, u32[]{:S(2)}) collective-permute-start(bf16[10640,128]{1,0:T(8,128)(2,1)} %get-tuple-element.36), channel_id=1, source_target_pairs={{0,2},{1,3},{2,0},{3,1},{4,6},{5,7},{6,4},{7,5}} | collective-permute-start | bytes 8171528 | tf_op jit(solution)/shard_map/ppermute | solution.py:692
  668.2 62.2 %collective-permute-start.1 = (bf16[10640,128]{1,0:T(8,128)(2,1)}, bf16[10640,128]{1,0:T(8,128)(2,1)S(1)}, u32[]{:S(2)}, u32[]{:S(2)}) collective-permute-start(bf16[10640,128]{1,0:T(8,128)(2,1)} %get-tuple-element.37), channel_id=1, source_target_pairs={{0,4},{1,5},{2,6},{3,7},{4,0},{5,1},{6,2},{7,3}} | collective-permute-start | bytes 8171528 | tf_op jit(solution)/shard_map/ppermute | solution.py:693
  669.4 23.3 %copy-start = (f32[8,6,128]{2,1,0:T(8,128)S(1)}, f32[8,6,128]{2,1,0:T(8,128)}, u32[]{:S(2)}) copy-start(f32[8,6,128]{2,1,0:T(8,128)} %get-tuple-element.42.vec_w) | copy-start | bytes 73732
  669.4 23.4 %copy-start.1 = (f32[3,6,128]{2,1,0:T(8,128)S(1)}, f32[3,6,128]{2,1,0:T(8,128)}, u32[]{:S(2)}) copy-start(f32[3,6,128]{2,1,0:T(8,128)} %get-tuple-element.41.vec_new) | copy-start | bytes 27652
  669.4 23.4 %copy-start.2 = (f32[8,128]{1,0:T(8,128)S(1)}, f32[8,128]{1,0:T(8,128)}, u32[]{:S(2)}) copy-start(f32[8,128]{1,0:T(8,128)} %get-tuple-element.39.coef) | copy-start | bytes 12292
  692.7 38.2 %copy-start.4 = (bf16[3360,128]{1,0:T(8,128)(2,1)S(1)}, bf16[3360,128]{1,0:T(8,128)(2,1)}, u32[]{:S(2)}) copy-start(bf16[3360,128]{1,0:T(8,128)(2,1)} %get-tuple-element.55) | copy-start | bytes 2580484
  692.7 39.0 %copy-start.3 = (bf16[3360,128]{1,0:T(8,128)(2,1)S(1)}, bf16[3360,128]{1,0:T(8,128)(2,1)}, u32[]{:S(2)}) copy-start(bf16[3360,128]{1,0:T(8,128)(2,1)} %get-tuple-element.56) | copy-start | bytes 2580484
  730.4 13.8 %collective-permute-start.4 = (bf16[10640,128]{1,0:T(8,128)(2,1)S(1)}, bf16[10640,128]{1,0:T(8,128)(2,1)S(1)}, u32[]{:S(2)}, u32[]{:S(2)}) collective-permute-start(bf16[10640,128]{1,0:T(8,128)(2,1)S(1)} %collective-permute-done.refs_1_), channel_id=1, source_target_pairs={{0,1},{1,0},{2,3},{3,2},{4,5},{5,4},{6,7},{7,6}} | collective-permute-start | bytes 8171528 | tf_op jit(solution)/shard_map/ppermute | solution.py:741
  730.4 13.7 %collective-permute-start.5 = (bf16[10640,128]{1,0:T(8,128)(2,1)S(1)}, bf16[10640,128]{1,0:T(8,128)(2,1)S(1)}, u32[]{:S(2)}, u32[]{:S(2)}) collective-permute-start(bf16[10640,128]{1,0:T(8,128)(2,1)S(1)} %collective-permute-done.1.refs_2_), channel_id=1, source_target_pairs={{0,1},{1,0},{2,3},{3,2},{4,5},{5,4},{6,7},{7,6}} | collective-permute-start | bytes 8171528 | tf_op jit(solution)/shard_map/ppermute | solution.py:742
  730.9 21.1 %collective-permute-start.2 = (bf16[3360,128]{1,0:T(8,128)(2,1)S(1)}, bf16[3360,128]{1,0:T(8,128)(2,1)S(1)}, u32[]{:S(2)}, u32[]{:S(2)}) collective-permute-start(bf16[3360,128]{1,0:T(8,128)(2,1)S(1)} %copy-done.4), channel_id=1, source_target_pairs={{0,2},{1,3},{2,0},{3,1},{4,6},{5,7},{6,4},{7,5}} | collective-permute-start | bytes 2580488 | tf_op jit(solution)/shard_map/ppermute | solution.py:694
  731.8 20.8 %collective-permute-start.3 = (bf16[3360,128]{1,0:T(8,128)(2,1)S(1)}, bf16[3360,128]{1,0:T(8,128)(2,1)S(1)}, u32[]{:S(2)}, u32[]{:S(2)}) collective-permute-start(bf16[3360,128]{1,0:T(8,128)(2,1)S(1)} %copy-done.3), channel_id=1, source_target_pairs={{0,4},{1,5},{2,6},{3,7},{4,0},{5,1},{6,2},{7,3}} | collective-permute-start | bytes 2580488 | tf_op jit(solution)/shard_map/ppermute | solution.py:695
  752.5 2.4 collective-permute-start.6
  752.5 3.6 collective-permute-start.7
